TPU v7x, 1024 devices: a whole 4x4x32 slice. The times are simulated.
1024 devices in a mesh: expert: 16 (over z_lo), dp: 64 (over x, y, z_hi, core).
Axes of the slice: x: 4, y: 4, z: 32 (z_hi: 2, z_lo: 16; z = z_hi * 16 + z_lo), core: 2. Of those that a mesh axis runs over, the one named last changes fastest.
Arguments:
- gradient: float32 [16, 64, 512, 1024], P('expert', 'dp'), may hold values from -200 to 200
- first_moment: float32 [16, 512, 1024], P('expert', 'dp'), may hold values from -0.6 to 0.6
- second_moment: float32 [16, 512, 1024], P('expert', 'dp'), may hold values from 0.002 to 0.02
- left_basis: float32 [16, 512, 512], P('expert'), may hold values from -1 to 1
- right_basis: float32 [16, 2, 512, 512], P('expert'), may hold values from -1 to 1
Outputs:
- update: float32 [16, 512, 1024], P('expert')
- new_first: float32 [16, 512, 1024], P('expert', 'dp')
- new_second: float32 [16, 512, 1024], P('expert', 'dp')
All inputs are finite; a program needn't handle non-finite values.
Results may differ from a plain program's by a relative error of at most 0.000092.
Values sent between devices are 32-bit elements; how exact they have to be, the bound alone decides.
No kernel may reach another device: no remote copies, remote signals or barrier semaphores. Data moves between devices by JAX's collectives and lax.ppermute only.
A program may use at most 32 MiB of HBM per device.

v0:
```python
import functools

import jax
import jax.numpy as jnp
from jax import lax
from jax.sharding import Mesh
from jax.sharding import PartitionSpec as P

DP = ("dp_0", "dp_1", "dp_2", "dp_3")
EXPERT_DP = ("expert", "dp_0", "dp_1", "dp_2", "dp_3")


highest = lax.Precision.HIGHEST


def in_blocks(x, dim, peers):
    shape = x.shape
    pieces = x.reshape(*shape[:dim], peers, shape[dim] // peers, *shape[dim + 1 :])
    return jnp.moveaxis(pieces, dim, 0)


def summed_rows(x, chips, core, dim):
    sizes = (lax.axis_size(chips), lax.axis_size(core))
    pieces = in_blocks(x, dim, sizes[0] * sizes[1])
    inside = pieces.shape[1:]
    pieces = pieces.reshape(*sizes, *inside).swapaxes(0, 1).reshape(-1, *inside)
    pieces = lax.psum_scatter(pieces, core, scatter_dimension=0, tiled=True)
    return lax.psum_scatter(pieces, chips, scatter_dimension=0, tiled=True)[0]


def over_axes(x, axes):
    return functools.reduce(lax.psum, axes, x)


def right_turn(values, basis):
    blocks = basis.shape[1]
    order = basis.shape[2]
    parts = values.reshape(values.shape[0], values.shape[1], blocks, order)
    out = jnp.einsum("erbc,ebcd->erbd", parts, basis, precision=highest)
    return out.reshape(values.shape)


def right_back(values, basis):
    blocks = basis.shape[1]
    order = basis.shape[2]
    parts = values.reshape(values.shape[0], values.shape[1], blocks, order)
    out = jnp.einsum("erbd,ebcd->erbc", parts, basis, precision=highest)
    return out.reshape(values.shape)


def per_device(gradient, first_moment, second_moment, left_basis, right_basis):
    local_grad = gradient[:, 0]
    experts, order, width = local_grad.shape
    replicas = lax.axis_size(DP)
    columns = left_basis
    partial_left = summed_rows(
        jnp.einsum("ekr,ekc->rec", columns, local_grad, precision=highest),
        ("dp_0", "dp_1", "dp_2"),
        "dp_3",
        0,
    )
    summed = right_turn(jnp.transpose(partial_left, (1, 0, 2)), right_basis)
    mean = summed / replicas
    new_first = 0.9 * first_moment + 0.1 * mean
    new_second = 0.95 * second_moment + 0.05 * mean * mean
    normal = new_first / (jnp.sqrt(new_second) + 1e-08)
    total = over_axes(jnp.sum(normal * normal), EXPERT_DP)
    count = experts * lax.axis_size("expert") * order * width
    scale = jnp.sqrt(total / count + 1e-06)
    turned = right_back(normal, right_basis)
    columns = left_basis
    back = jnp.einsum(
        "ekr,erc->ekc", columns, lax.all_gather(turned, DP, axis=1, tiled=True), precision=highest
    )
    return (back / scale, new_first, new_second)


def solution(mesh):
    split = Mesh(
        mesh.devices.reshape(mesh.shape["expert"], 4, 4, 2, 2),
        ("expert", "dp_0", "dp_1", "dp_2", "dp_3"),
    )
    in_specs = (
        P("expert", DP, None, None),
        P("expert", DP, None),
        P("expert", DP, None),
        P("expert", None, None),
        P("expert", None, None, None),
    )
    out_specs = (P("expert", None, None), P("expert", DP, None), P("expert", DP, None))
    return jax.shard_map(
        per_device, mesh=split, in_specs=in_specs, out_specs=out_specs, check_vma=False
    )
```

profile of v0, /device:TPU:1, one launch (start us, length us, event | category | flops | bytes accessed | tf_op | source)
XLA Modules:
  0.0 794.5 jit_solution(18053659251817439606)
XLA Ops:
  7.2 0.0 copy-start
  7.2 0.0 reduce-scatter.3.cloned.1.call-start
  7.2 1.5 copy-done
  8.8 4.8 fusion.6
  13.5 1.5 copy.9
  15.0 0.0 reduce-scatter.3.cloned.1.call-update
  15.0 0.0 reduce-scatter.5.cloned.1.call-start
  15.1 41.3 %reduce-scatter.3.cloned.1.call-done = f32[32,8,1,1024]{3,1,0,2:T(8,128)} async-done(((f32[64,8,1,1024]{3,1,0,2:T(8,128)}), f32[32,8,1,1024]{3,1,0,2:T(8,128)}) %reduce-scatter.3.cloned.1.call-update) | async-done | bytes 1048592 | tf_op jit(solution)/shard_map/reduce_scatter | solution.py:27
  56.4 0.0 reduce-scatter.5.cloned.1.call-update
  56.4 0.0 all-gather.2.cloned.1.call-start
  56.5 497.7 %reduce-scatter.5.cloned.1.call-done = f32[1,8,1,1024]{3,1,0,2:T(8,128)} async-done(((f32[32,8,1,1024]{3,1,0,2:T(8,128)}), f32[1,8,1,1024]{3,1,0,2:T(8,128)}) %reduce-scatter.5.cloned.1.call-update) | async-done | bytes 32784 | tf_op jit(solution)/shard_map/reduce_scatter | solution.py:28
  554.1 2.9 broadcast_multiply_fusion
  557.0 0.0 copy-done.3
  557.0 1.2 multiply_reduce_fusion
  558.2 2.4 fusion.2
  560.7 0.0 all-gather.2.cloned.1.call-update
  560.7 81.7 %psum.35 = f32[]{:T(128)} all-reduce(f32[]{:T(128)} %get-tuple-element.9), channel_id=1, replica_groups=mesh['expert'=16,'dp_0'=4,'dp_1'=4,'dp_2'=2,'dp_3'=2] {'expert'}, use_global_device_ids=true, to_apply=%region_3.0 | all-reduce | flops 1 | bytes 8 | tf_op jit(solution)/shard_map/psum | solution.py:32
  642.4 13.5 %psum.36 = f32[]{:T(128)} all-reduce(f32[]{:T(128)} %psum.35), channel_id=1, replica_groups=mesh['expert'=16,'dp_0'=4,'dp_1'=4,'dp_2'=2,'dp_3'=2] {'dp_0'}, use_global_device_ids=true, to_apply=%region_4.0 | all-reduce | flops 1 | bytes 8 | tf_op jit(solution)/shard_map/psum | solution.py:32
  655.9 7.3 psum.37
  663.3 22.8 %psum.38 = f32[]{:T(128)} all-reduce(f32[]{:T(128)} %psum.37), channel_id=1, replica_groups=mesh['expert'=16,'dp_0'=4,'dp_1'=4,'dp_2'=2,'dp_3'=2] {'dp_2'}, use_global_device_ids=true, to_apply=%region_6.0 | all-reduce | flops 1 | bytes 8 | tf_op jit(solution)/shard_map/psum | solution.py:32
  686.1 81.4 %psum.39 = f32[]{:T(128)} all-reduce(f32[]{:T(128)} %psum.38), channel_id=1, replica_groups=mesh['expert'=16,'dp_0'=4,'dp_1'=4,'dp_2'=2,'dp_3'=2] {'dp_3'}, use_global_device_ids=true, to_apply=%region_7.0 | all-reduce | flops 1 | bytes 8 | tf_op jit(solution)/shard_map/psum | solution.py:32
  768.1 7.4 all-gather.2.cloned.1.call-done
  775.6 9.6 %divide_bitcast_fusion = f32[1,512,1024]{1,2,0:T(8,128)} fusion(f32[1,512,1024]{2,1,0:T(8,128)} %all-gather.2.cloned.1.call-done, f32[1,512,512]{2,1,0:T(8,128)S(1)} %copy-done.2, f32[]{:T(128)S(6)} %sqrt.7), kind=kOutput, calls=%fused_computation.8 | convolution fusion | flops 3221749760 | bytes 5242884 | tf_op jit(solution)/shard_map/ekr,erc->ekc/dot_general | solution.py:72
  785.1 2.9 copy.11
  (7 shorter events, 0.0 us)
Async XLA Ops:
  7.2 1.6 copy-start
  7.2 49.2 %reduce-scatter.3.cloned.1.call-start = ((), (), s32[]{:S(2)}) async-start(), calls=%async_computation.2 | async-start | bytes 3145728 | tf_op jit(solution)/shard_map/reduce_scatter | solution.py:27
  15.0 541.9 %copy-start.3 = (f32[1,8,1024]{2,1,0:T(8,128)S(1)}, f32[1,8,1024]{2,1,0:T(8,128)}, u32[]{:S(2)}) copy-start(f32[1,8,1024]{2,1,0:T(8,128)} %param.7) | copy-start | bytes 98308
  15.0 541.9 %copy-start.4 = (f32[1,8,1024]{2,1,0:T(8,128)S(1)}, f32[1,8,1024]{2,1,0:T(8,128)}, u32[]{:S(2)}) copy-start(f32[1,8,1024]{2,1,0:T(8,128)} %param.6) | copy-start | bytes 98308
  15.0 539.1 %reduce-scatter.5.cloned.1.call-start = ((), (), s32[]{:S(2)}) async-start(), calls=%async_computation.3 | async-start | bytes 1081344 | tf_op jit(solution)/shard_map/reduce_scatter | solution.py:28
  56.4 719.2 %all-gather.2.cloned.1.call-start = ((), (), s32[]{:S(2)}) async-start(), calls=%async_computation.4 | async-start | bytes 2129920 | tf_op jit(solution)/shard_map/all_gather | solution.py:73
  554.1 4.1 copy-start.1
  554.1 221.5 %copy-start.2 = (f32[1,512,512]{2,1,0:T(8,128)S(1)}, f32[1,512,512]{2,1,0:T(8,128)}, u32[]{:S(2)}) copy-start(f32[1,512,512]{2,1,0:T(8,128)} %param.8) | copy-start | bytes 3145732
Sparse Core Ops, SparseCore 0:
  15.1 41.1 reduce-scatter.2
  59.8 494.3 reduce-scatter.4
  560.8 214.6 all-gather.1
where the time goes:
time: 795 us
  waiting for transfers between devices  546 us (69%)
  blocking collectives  207 us (26%)
  matrix products  19.6 us (2%)
  between operations  14.5 us (2%)
    reduce_scatter x1, waiting for transfers between devices, summed_rows(): return lax.psum_scatter(pieces, chips, scatter_dimension=0, tiled=True)[0]  498 us
    psum x5, blocking collectives, over_axes(): return functools.reduce(lax.psum, axes, x)  207 us
    reduce_scatter x1, waiting for transfers between devices, summed_rows(): pieces = lax.psum_scatter(pieces, core, scatter_dimension=0, tiled=True)  41.3 us
  transfers between devices with their start and end apart: 3, of which 3 were waited for; matrix products, arithmetic and copies ran while one was open for 0% of the time, Pallas kernels for 0%

commit v1 on v0

v1 whole, which is shorter than its diff:
```python
import jax
import jax.numpy as jnp
from jax import lax
from jax.sharding import Mesh
from jax.sharding import PartitionSpec as P


DP = ("dp_0", "dp_1", "dp_2", "dp_3")
PLANE = ("dp_0", "dp_1")
PLANE_CORE = ("dp_0", "dp_1", "dp_3")
RING = ("expert", "dp_2")
SWAP = [(0, 1), (1, 0)]

highest = lax.Precision.HIGHEST


def rows_dot(a, b):
    return lax.dot_general(a, b, (((0,), (0,)), ((), ())), precision=highest)


def right_turn(values, basis):
    blocks, order = basis.shape[0], basis.shape[1]
    parts = values.reshape(values.shape[0], blocks, order)
    out = jnp.einsum("rbc,bcd->rbd", parts, basis, precision=highest)
    return out.reshape(values.shape)


def right_back(values, basis):
    blocks, order = basis.shape[0], basis.shape[1]
    parts = values.reshape(values.shape[0], blocks, order)
    out = jnp.einsum("rbd,bcd->rbc", parts, basis, precision=highest)
    return out.reshape(values.shape)


def shared_total(tile, axes):
    tiles = jnp.broadcast_to(tile, (lax.axis_size(axes), *tile.shape))
    return jnp.sum(lax.all_to_all(tiles, axes, 0, 0), axis=0)


def along_z(tile, steps):
    ring, experts = lax.axis_size(RING), lax.axis_size("expert")
    place = [z % experts * (ring // experts) + z // experts for z in range(ring)]
    moved = [
        lax.ppermute(tile, RING, [(place[z], place[(z + step) % ring]) for z in range(ring)])
        for step in steps
    ]
    return sum(moved, tile)


def halves(own, other, index):
    return jnp.concatenate(
        (jnp.where(index == 0, own, other), jnp.where(index == 0, other, own)), axis=0
    )


def per_device(gradient, first_moment, second_moment, left_basis, right_basis):
    left, right = left_basis[0], right_basis[0]
    local = gradient[0, 0]
    order, width = local.shape
    replicas = lax.axis_size(DP)
    chips = lax.axis_size(PLANE)
    rows = first_moment.shape[1]
    half = lax.axis_index("dp_2")
    core = lax.axis_index("dp_3")

    columns = jnp.transpose(left).reshape(-1, 2, rows, order)
    here = lax.dynamic_index_in_dim(columns, core, 1, keepdims=False).reshape(-1, order)
    there = lax.dynamic_index_in_dim(columns, 1 - core, 1, keepdims=False).reshape(-1, order)
    sent = jnp.dot(there, local, precision=highest)
    kept = lax.optimization_barrier(jnp.dot(here, local, precision=highest))
    pair = kept + lax.ppermute(sent, "dp_3", SWAP)
    pieces = lax.all_to_all(pair.reshape(chips, 2 * rows, width), PLANE, 0, 0)
    partial = jnp.sum(pieces, axis=0)

    moments = jnp.concatenate((first_moment[0], second_moment[0]), axis=0)
    moments_there = lax.ppermute(moments, "dp_2", SWAP)
    first = halves(first_moment[0], moments_there[:rows], half)
    second = halves(second_moment[0], moments_there[rows:], half)

    summed = partial + lax.ppermute(partial, "dp_2", SWAP)
    mean = right_turn(summed, right) / replicas
    new_first = 0.9 * first + 0.1 * mean
    new_second = 0.95 * second + 0.05 * mean * mean
    normal = new_first / (jnp.sqrt(new_second) + 1e-08)

    squares = jnp.broadcast_to(jnp.sum(normal * normal), (8, 128))
    expert_total = shared_total(squares, PLANE_CORE)
    turned, expert_total = lax.optimization_barrier((right_back(normal, right), expert_total))
    total = along_z(along_z(expert_total, (1, -1, 2)), (4, -4, 8))[0, 0]
    count = lax.axis_size("expert") * order * width
    scale = jnp.sqrt(total / count + 1e-06)
    ours = lax.all_to_all(jnp.broadcast_to(turned, (chips, 2 * rows, width)), PLANE, 0, 0)
    ours = ours.reshape(-1, width)
    theirs = lax.ppermute(ours, "dp_3", SWAP)
    back = rows_dot(here, ours) + rows_dot(there, theirs)
    own = lambda x: lax.dynamic_slice_in_dim(x, half * rows, rows, 0)
    return ((back / scale)[None], own(new_first)[None], own(new_second)[None])


def solution(mesh):
    split = Mesh(
        mesh.devices.reshape(mesh.shape["expert"], 4, 4, 2, 2),
        ("expert", "dp_0", "dp_1", "dp_2", "dp_3"),
    )
    in_specs = (
        P("expert", DP, None, None),
        P("expert", DP, None),
        P("expert", DP, None),
        P("expert", None, None),
        P("expert", None, None, None),
    )
    out_specs = (P("expert", None, None), P("expert", DP, None), P("expert", DP, None))
    return jax.shard_map(
        per_device, mesh=split, in_specs=in_specs, out_specs=out_specs, check_vma=False
    )
```

time: 795 us -> 156 us (0.20)
  waiting for transfers between devices: 546 us -> 23.9 us
  blocking collectives: 207 us -> 0 us
  starting transfers between devices: 0.12 us -> 101 us
  between operations: 14.5 us -> 1.62 us
    reduce_scatter x2 -> x0, waiting for transfers between devices: 539 us -> none  [the longest x1 498 us: summed_rows(): return lax.psum_scatter(pieces, chips, scatter_dimension=0, tiled=True)[0]]
    psum x5 -> x0, blocking collectives: 207 us -> none  [over_axes(): return functools.reduce(lax.psum, axes, x)]
    ppermute x0 -> x10, starting transfers between devices: none -> 76.5 us  [the longest x6 22 us: along_z(): lax.ppermute(tile, RING, [(place[z], place[(z + step) % ring]) for z in r...]
    all_to_all x0 -> x3, starting transfers between devices: none -> 24.7 us  [the longest x1 16.1 us: shared_total(): return jnp.sum(lax.all_to_all(tiles, axes, 0, 0), axis=0)]
    ppermute x0 -> x10, waiting for transfers between devices: none -> 14.1 us  [the longest x1 8.18 us: per_device(): summed = partial + lax.ppermute(partial, 'dp_2', SWAP)]
    all_to_all x0 -> x3, waiting for transfers between devices: none -> 9.83 us  [the longest x1 5.56 us: per_device(): lax.all_to_all(jnp.broadcast_to(turned, (chips, 2 * rows, width)), PLANE,...]
    dot_general x4 -> x6, matrix products: 19.6 us -> 17.9 us  [the longest x2 6.42 us: rows_dot(): return lax.dot_general(a, b, (((0,), (0,)), ((), ())), precision=highest)]
  transfers between devices with their start and end apart: 3 -> 13, of which waited for: 3 -> 6; matrix products, arithmetic and copies ran while one was open for 0% -> 7% of each run, Pallas kernels for 0% -> 0%
where the time goes in v1:
time: 156 us; the launch traced here: 154 us
  starting transfers between devices  101 us (65%)
  waiting for transfers between devices  23.9 us (15%)
  matrix products  17.9 us (11%)
  local copies, waits for them, and re-layouts  4.84 us (3%)
  other arithmetic  4.37 us (3%)
  between operations  1.62 us (1%)
    ppermute x6, starting transfers between devices, along_z(): lax.ppermute(tile, RING, [(place[z], place[(z + step) % ring]) for z in r...  22 us
    ppermute x1, starting transfers between devices, per_device(): moments_there = lax.ppermute(moments, 'dp_2', SWAP)  18.5 us
    all_to_all x1, starting transfers between devices, shared_total(): return jnp.sum(lax.all_to_all(tiles, axes, 0, 0), axis=0)  16.1 us
    ppermute x1, starting transfers between devices, per_device(): pair = kept + lax.ppermute(sent, 'dp_3', SWAP)  16 us
    ppermute x1, starting transfers between devices, per_device(): summed = partial + lax.ppermute(partial, 'dp_2', SWAP)  15.6 us
    ppermute x1, waiting for transfers between devices, per_device(): summed = partial + lax.ppermute(partial, 'dp_2', SWAP)  8.18 us
    dot_general x2, matrix products, rows_dot(): return lax.dot_general(a, b, (((0,), (0,)), ((), ())), precision=highest)  6.42 us
    all_to_all x1, waiting for transfers between devices, per_device(): lax.all_to_all(jnp.broadcast_to(turned, (chips, 2 * rows, width)), PLANE,...  5.56 us
  transfers between devices with their start and end apart: 13, of which 6 were waited for; matrix products, arithmetic and copies ran while one was open for 7% of the time, Pallas kernels for 0%

profile of v1, /device:TPU:1, one launch (start us, length us, event | category | flops | bytes accessed | tf_op | source)
XLA Modules:
  0.0 153.9 jit_solution(14413021266856311478)
XLA Ops:
  2.5 2.9 %fusion.4 = f32[256,1024]{1,0:T(8,128)} fusion(f32[1,1,512,1024]{3,2,1,0:T(8,128)S(1)} %copy-done, f32[32,2,8,512]{3,2,1,0:T(8,128)S(1)} %bitcast.73, s32[]{:T(128)S(6)} %select_n.35), kind=kOutput, calls=%fused_computation.4 | convolution fusion | flops 1610612736 | bytes 3670020 | tf_op jit(solution)/shard_map/dot_general | solution.py:69
  5.4 16.0 %collective-permute-start.1 = (f32[256,1024]{1,0:T(8,128)}, f32[256,1024]{1,0:T(8,128)}, u32[]{:S(2)}, u32[]{:S(2)}) collective-permute-start(f32[256,1024]{1,0:T(8,128)} %fusion.4), channel_id=1, source_target_pairs={{0,1},{1,0},{2,3},{3,2},{4,5},{5,4},{6,7},{7,6},{8,9},{9,8},{10,11... | collective-permute-start | bytes 3145736 | tf_op jit(solution)/shard_map/ppermute | solution.py:71
  21.4 1.9 %fusion.6 = f32[256,1024]{1,0:T(8,128)S(1)} fusion(f32[1,1,512,1024]{3,2,1,0:T(8,128)S(1)} %copy-done, f32[32,2,8,512]{3,2,1,0:T(8,128)S(1)} %bitcast.74, s32[]{:T(128)S(6)} %select_n.31), kind=kOutput, calls=%fused_computation.6 | convolution fusion | flops 1610612736 | bytes 3670020 | tf_op jit(solution)/shard_map/dot_general | solution.py:70
  24.0 2.3 %add.67 = f32[256,1024]{1,0:T(8,128)} add(f32[256,1024]{1,0:T(8,128)S(1)} %fusion.6, f32[256,1024]{1,0:T(8,128)} %collective-permute-done.1) | non-fusion elementwise | flops 262144 | bytes 3145728 | tf_op jit(solution)/shard_map/add | solution.py:71
  26.4 4.3 %all-to-all-start = ((f32[16,16,1024]{2,1,0:T(8,128)}), f32[16,16,1024]{2,1,0:T(8,128)}, u32[]{:S(2)}, u32[]{:S(2)}) async-start(f32[16,16,1024]{2,1,0:T(8,128)} %bitcast.77), calls=%async_computation | async-start | bytes 2097152 | tf_op jit(solution)/shard_map/all_to_all | solution.py:72
  30.7 18.5 %collective-permute-start = (f32[16,1024]{1,0:T(8,128)S(1)}, f32[16,1024]{1,0:T(8,128)S(1)}, u32[]{:S(2)}, u32[]{:S(2)}) collective-permute-start(f32[16,1024]{1,0:T(8,128)S(1)} %pad_maximum_fusion), channel_id=1, source_target_pairs={{0,2},{2,0},{1,3},{3,1},{4,6},{6,4},{5,7},{7,5},{8,10},{10,8},{9,1... | collective-permute-start | bytes 196616 | tf_op jit(solution)/shard_map/ppermute | solution.py:76
  50.6 15.6 %collective-permute-start.2 = (f32[16,1024]{1,0:T(8,128)S(1)}, f32[16,1024]{1,0:T(8,128)S(1)}, u32[]{:S(2)}, u32[]{:S(2)}) collective-permute-start(f32[16,1024]{1,0:T(8,128)S(1)} %reduce_sum.27), channel_id=1, source_target_pairs={{0,2},{2,0},{1,3},{3,1},{4,6},{6,4},{5,7},{7,5},{8,10},{10,8},{9,1... | collective-permute-start | bytes 196616 | tf_op jit(solution)/shard_map/ppermute | solution.py:80
  66.3 8.2 %collective-permute-done.2 = f32[16,1024]{1,0:T(8,128)S(1)} collective-permute-done((f32[16,1024]{1,0:T(8,128)S(1)}, f32[16,1024]{1,0:T(8,128)S(1)}, u32[]{:S(2)}, u32[]{:S(2)}) %collective-permute-start.2) | collective-permute-done | bytes 65568 | tf_op jit(solution)/shard_map/ppermute | solution.py:80
  74.5 3.3 %multiply_reduce_fusion = (f32[]{:T(128)}, f32[16,2,512]{2,0,1:T(8,128)S(1)}, f32[2,16,512]{2,1,0:T(8,128)S(1)}) fusion(f32[8,2,512]{2,0,1:T(8,128)S(1)} %bitcast.80, f32[8,2,512]{2,0,1:T(8,128)S(1)} %bitcast.81, f32[8,2,512]{2,0,1:T(8,128)S(1)} %bitcast.79, f32[8,2,512]{2,0,1:T(8,128)S(1)} %bitcast.78, f32[1,2,512,512]{3,2,1,0:T(8,128)} %param.9, ...), kind=kOutput, calls=%fused_computation.33 | convolution fusion | flops 100892672 | bytes 2424836 | tf_op jit(solution)/shard_map/rbc,bcd->rbd/dot_general | solution.py:24
  79.1 16.1 %all-to-all-start.1 = ((f32[32,8,128]{2,1,0:T(8,128)}), f32[32,8,128]{2,1,0:T(8,128)S(1)}, u32[]{:S(2)}, u32[]{:S(2)}) async-start(f32[32,8,128]{2,1,0:T(8,128)} %broadcast_in_dim_broadcast_in_dim.3), calls=%async_computation.1 | async-start | bytes 262144 | tf_op jit(solution)/shard_map/all_to_all | solution.py:37
  95.2 3.4 %fusion.8 = f32[2,2,8,512]{3,2,1,0:T(8,128)S(1)} fusion(f32[16,2,512]{2,0,1:T(8,128)S(1)} %get-tuple-element.8, f32[1,2,512,512]{3,2,1,0:T(8,128)} %param.9), kind=kOutput, calls=%fused_computation.9 | convolution fusion | flops 100663296 | bytes 2228224 | tf_op jit(solution)/shard_map/rbd,bcd->rbc/dot_general | solution.py:31
  98.6 4.3 %all-to-all-done.1 = f32[32,8,128]{2,1,0:T(8,128)S(1)} async-done(((f32[32,8,128]{2,1,0:T(8,128)}), f32[32,8,128]{2,1,0:T(8,128)S(1)}, u32[]{:S(2)}, u32[]{:S(2)}) %all-to-all-start.1) | async-done | bytes 131104 | tf_op jit(solution)/shard_map/all_to_all | solution.py:37
  104.0 4.3 %all-to-all-start.2 = ((f32[16,16,1024]{2,1,0:T(8,128)}), f32[16,16,1024]{2,1,0:T(8,128)}, u32[]{:S(2)}, u32[]{:S(2)}) async-start(f32[16,16,1024]{2,1,0:T(8,128)} %broadcast_in_dim.12), calls=%async_computation.2 | async-start | bytes 2097152 | tf_op jit(solution)/shard_map/all_to_all | solution.py:92
  108.3 4.0 %collective-permute-start.6 = (f32[8,128]{1,0:T(8,128)S(1)}, f32[8,128]{1,0:T(8,128)S(1)}, u32[]{:S(2)}, u32[]{:S(2)}) collective-permute-start(f32[8,128]{1,0:T(8,128)S(1)} %reduce_sum.29), channel_id=1, source_target_pairs={{0,128},{64,192},{128,256},{192,320},{256,384},{320,448},{384,512}... | collective-permute-start | bytes 12296 | tf_op jit(solution)/shard_map/ppermute | solution.py:44
  112.4 4.8 %collective-permute-start.5 = (f32[8,128]{1,0:T(8,128)S(1)}, f32[8,128]{1,0:T(8,128)S(1)}, u32[]{:S(2)}, u32[]{:S(2)}) collective-permute-start(f32[8,128]{1,0:T(8,128)S(1)} %reduce_sum.29), channel_id=1, source_target_pairs={{0,962},{64,0},{128,64},{192,128},{256,192},{320,256},{384,320},{4... | collective-permute-start | bytes 12296 | tf_op jit(solution)/shard_map/ppermute | solution.py:44
  117.1 1.9 %collective-permute-start.4 = (f32[8,128]{1,0:T(8,128)S(1)}, f32[8,128]{1,0:T(8,128)S(1)}, u32[]{:S(2)}, u32[]{:S(2)}) collective-permute-start(f32[8,128]{1,0:T(8,128)S(1)} %reduce_sum.29), channel_id=1, source_target_pairs={{0,64},{64,128},{128,192},{192,256},{256,320},{320,384},{384,448},... | collective-permute-start | bytes 12296 | tf_op jit(solution)/shard_map/ppermute | solution.py:44
  119.1 5.6 %all-to-all-done.2 = f32[16,16,1024]{2,1,0:T(8,128)} async-done(((f32[16,16,1024]{2,1,0:T(8,128)}), f32[16,16,1024]{2,1,0:T(8,128)}, u32[]{:S(2)}, u32[]{:S(2)}) %all-to-all-start.2) | async-done | bytes 1048608 | tf_op jit(solution)/shard_map/all_to_all | solution.py:92
  124.6 4.4 %collective-permute-start.3 = (f32[256,1024]{1,0:T(8,128)}, f32[256,1024]{1,0:T(8,128)S(1)}, u32[]{:S(2)}, u32[]{:S(2)}) collective-permute-start(f32[256,1024]{1,0:T(8,128)} %bitcast.19), channel_id=1, source_target_pairs={{0,1},{1,0},{2,3},{3,2},{4,5},{5,4},{6,7},{7,6},{8,9},{9,8},{10,11... | collective-permute-start | bytes 3145736 | tf_op jit(solution)/shard_map/ppermute | solution.py:94
  129.1 1.9 %collective-permute-start.9 = (f32[8,128]{1,0:T(8,128)S(1)}, f32[8,128]{1,0:T(8,128)S(1)}, u32[]{:S(2)}, u32[]{:S(2)}) collective-permute-start(f32[8,128]{1,0:T(8,128)S(1)} %add_add_fusion.1), channel_id=1, source_target_pairs={{0,512},{64,576},{128,640},{192,704},{256,768},{320,832},{384,896}... | collective-permute-start | bytes 12296 | tf_op jit(solution)/shard_map/ppermute | solution.py:44
  131.0 6.2 %collective-permute-start.8 = (f32[8,128]{1,0:T(8,128)S(1)}, f32[8,128]{1,0:T(8,128)S(1)}, u32[]{:S(2)}, u32[]{:S(2)}) collective-permute-start(f32[8,128]{1,0:T(8,128)S(1)} %add_add_fusion.1), channel_id=1, source_target_pairs={{0,770},{64,834},{128,898},{192,962},{256,0},{320,64},{384,128},{4... | collective-permute-start | bytes 12296 | tf_op jit(solution)/shard_map/ppermute | solution.py:44
  137.2 3.2 %collective-permute-start.7 = (f32[8,128]{1,0:T(8,128)S(1)}, f32[8,128]{1,0:T(8,128)S(1)}, u32[]{:S(2)}, u32[]{:S(2)}) collective-permute-start(f32[8,128]{1,0:T(8,128)S(1)} %add_add_fusion.1), channel_id=1, source_target_pairs={{0,256},{64,320},{128,384},{192,448},{256,512},{320,576},{384,640}... | collective-permute-start | bytes 12296 | tf_op jit(solution)/shard_map/ppermute | solution.py:44
  142.2 4.1 %collective-permute-done.7 = f32[8,128]{1,0:T(8,128)S(1)} collective-permute-done((f32[8,128]{1,0:T(8,128)S(1)}, f32[8,128]{1,0:T(8,128)S(1)}, u32[]{:S(2)}, u32[]{:S(2)}) %collective-permute-start.7) | collective-permute-done | bytes 4128 | tf_op jit(solution)/shard_map/ppermute | solution.py:44
  147.5 3.1 %fusion.13 = f32[512,1024]{1,0:T(8,128)S(1)} fusion(f32[256,1024]{1,0:T(8,128)} %bitcast.19, f32[32,2,8,512]{3,2,1,0:T(8,128)S(1)} %bitcast.75, s32[]{:T(128)S(6)} %select_n.31), kind=kOutput, calls=%fused_computation.12 | convolution fusion | flops 1610612736 | bytes 3670020 | tf_op jit(solution)/shard_map/dot_general | solution.py:18
  150.6 3.3 %divide_bitcast_fusion = f32[1,512,1024]{2,1,0:T(8,128)} fusion(f32[512,1024]{1,0:T(8,128)S(1)} %fusion.13, f32[256,1024]{1,0:T(8,128)S(1)} %collective-permute-done.3, f32[]{:T(128)} %bitcast.20, f32[32,2,8,512]{3,2,1,0:T(8,128)S(1)} %bitcast.76, s32[]{:T(128)S(6)} %select_n.35), kind=kOutput, calls=%fused_computation.8 | convolution fusion | flops 1611661312 | bytes 5767176 | tf_op jit(solution)/shard_map/dot_general | solution.py:18
  (31 shorter events, 8.7 us)
Async XLA Ops:
  0.6 1.9 %copy-start = (f32[1,1,512,1024]{3,2,1,0:T(8,128)S(1)}, f32[1,1,512,1024]{3,2,1,0:T(8,128)}, u32[]{:S(2)}) copy-start(f32[1,1,512,1024]{3,2,1,0:T(8,128)} %param.5) | copy-start | bytes 6291460
  5.4 18.6 %collective-permute-start.1 = (f32[256,1024]{1,0:T(8,128)}, f32[256,1024]{1,0:T(8,128)}, u32[]{:S(2)}, u32[]{:S(2)}) collective-permute-start(f32[256,1024]{1,0:T(8,128)} %fusion.4), channel_id=1, source_target_pairs={{0,1},{1,0},{2,3},{3,2},{4,5},{5,4},{6,7},{7,6},{8,9},{9,8},{10,11... | collective-permute-start | bytes 3145736 | tf_op jit(solution)/shard_map/ppermute | solution.py:71
  23.3 7.4 %copy-start.1 = (f32[1,8,1024]{2,1,0:T(8,128)S(1)}, f32[1,8,1024]{2,1,0:T(8,128)}, u32[]{:S(2)}) copy-start(f32[1,8,1024]{2,1,0:T(8,128)} %param.7) | copy-start | bytes 98308
  23.3 7.4 %copy-start.2 = (f32[1,8,1024]{2,1,0:T(8,128)S(1)}, f32[1,8,1024]{2,1,0:T(8,128)}, u32[]{:S(2)}) copy-start(f32[1,8,1024]{2,1,0:T(8,128)} %param.6) | copy-start | bytes 98308
  26.4 22.9 %all-to-all-start = ((f32[16,16,1024]{2,1,0:T(8,128)}), f32[16,16,1024]{2,1,0:T(8,128)}, u32[]{:S(2)}, u32[]{:S(2)}) async-start(f32[16,16,1024]{2,1,0:T(8,128)} %bitcast.77), calls=%async_computation | async-start | bytes 2097152 | tf_op jit(solution)/shard_map/all_to_all | solution.py:72
  30.7 35.5 %collective-permute-start = (f32[16,1024]{1,0:T(8,128)S(1)}, f32[16,1024]{1,0:T(8,128)S(1)}, u32[]{:S(2)}, u32[]{:S(2)}) collective-permute-start(f32[16,1024]{1,0:T(8,128)S(1)} %pad_maximum_fusion), channel_id=1, source_target_pairs={{0,2},{2,0},{1,3},{3,1},{4,6},{6,4},{5,7},{7,5},{8,10},{10,8},{9,1... | collective-permute-start | bytes 196616 | tf_op jit(solution)/shard_map/ppermute | solution.py:76
  50.6 23.9 %collective-permute-start.2 = (f32[16,1024]{1,0:T(8,128)S(1)}, f32[16,1024]{1,0:T(8,128)S(1)}, u32[]{:S(2)}, u32[]{:S(2)}) collective-permute-start(f32[16,1024]{1,0:T(8,128)S(1)} %reduce_sum.27), channel_id=1, source_target_pairs={{0,2},{2,0},{1,3},{3,1},{4,6},{6,4},{5,7},{7,5},{8,10},{10,8},{9,1... | collective-permute-start | bytes 196616 | tf_op jit(solution)/shard_map/ppermute | solution.py:80
  79.1 23.7 %all-to-all-start.1 = ((f32[32,8,128]{2,1,0:T(8,128)}), f32[32,8,128]{2,1,0:T(8,128)S(1)}, u32[]{:S(2)}, u32[]{:S(2)}) async-start(f32[32,8,128]{2,1,0:T(8,128)} %broadcast_in_dim_broadcast_in_dim.3), calls=%async_computation.1 | async-start | bytes 262144 | tf_op jit(solution)/shard_map/all_to_all | solution.py:37
  104.0 20.6 %all-to-all-start.2 = ((f32[16,16,1024]{2,1,0:T(8,128)}), f32[16,16,1024]{2,1,0:T(8,128)}, u32[]{:S(2)}, u32[]{:S(2)}) async-start(f32[16,16,1024]{2,1,0:T(8,128)} %broadcast_in_dim.12), calls=%async_computation.2 | async-start | bytes 2097152 | tf_op jit(solution)/shard_map/all_to_all | solution.py:92
  108.3 20.7 %collective-permute-start.6 = (f32[8,128]{1,0:T(8,128)S(1)}, f32[8,128]{1,0:T(8,128)S(1)}, u32[]{:S(2)}, u32[]{:S(2)}) collective-permute-start(f32[8,128]{1,0:T(8,128)S(1)} %reduce_sum.29), channel_id=1, source_target_pairs={{0,128},{64,192},{128,256},{192,320},{256,384},{320,448},{384,512}... | collective-permute-start | bytes 12296 | tf_op jit(solution)/shard_map/ppermute | solution.py:44
  112.4 16.7 %collective-permute-start.5 = (f32[8,128]{1,0:T(8,128)S(1)}, f32[8,128]{1,0:T(8,128)S(1)}, u32[]{:S(2)}, u32[]{:S(2)}) collective-permute-start(f32[8,128]{1,0:T(8,128)S(1)} %reduce_sum.29), channel_id=1, source_target_pairs={{0,962},{64,0},{128,64},{192,128},{256,192},{320,256},{384,320},{4... | collective-permute-start | bytes 12296 | tf_op jit(solution)/shard_map/ppermute | solution.py:44
  117.1 11.9 %collective-permute-start.4 = (f32[8,128]{1,0:T(8,128)S(1)}, f32[8,128]{1,0:T(8,128)S(1)}, u32[]{:S(2)}, u32[]{:S(2)}) collective-permute-start(f32[8,128]{1,0:T(8,128)S(1)} %reduce_sum.29), channel_id=1, source_target_pairs={{0,64},{64,128},{128,192},{192,256},{256,320},{320,384},{384,448},... | collective-permute-start | bytes 12296 | tf_op jit(solution)/shard_map/ppermute | solution.py:44
  124.6 26.0 %collective-permute-start.3 = (f32[256,1024]{1,0:T(8,128)}, f32[256,1024]{1,0:T(8,128)S(1)}, u32[]{:S(2)}, u32[]{:S(2)}) collective-permute-start(f32[256,1024]{1,0:T(8,128)} %bitcast.19), channel_id=1, source_target_pairs={{0,1},{1,0},{2,3},{3,2},{4,5},{5,4},{6,7},{7,6},{8,9},{9,8},{10,11... | collective-permute-start | bytes 3145736 | tf_op jit(solution)/shard_map/ppermute | solution.py:94
  129.1 13.1 %collective-permute-start.9 = (f32[8,128]{1,0:T(8,128)S(1)}, f32[8,128]{1,0:T(8,128)S(1)}, u32[]{:S(2)}, u32[]{:S(2)}) collective-permute-start(f32[8,128]{1,0:T(8,128)S(1)} %add_add_fusion.1), channel_id=1, source_target_pairs={{0,512},{64,576},{128,640},{192,704},{256,768},{320,832},{384,896}... | collective-permute-start | bytes 12296 | tf_op jit(solution)/shard_map/ppermute | solution.py:44
  131.0 11.1 %collective-permute-start.8 = (f32[8,128]{1,0:T(8,128)S(1)}, f32[8,128]{1,0:T(8,128)S(1)}, u32[]{:S(2)}, u32[]{:S(2)}) collective-permute-start(f32[8,128]{1,0:T(8,128)S(1)} %add_add_fusion.1), channel_id=1, source_target_pairs={{0,770},{64,834},{128,898},{192,962},{256,0},{320,64},{384,128},{4... | collective-permute-start | bytes 12296 | tf_op jit(solution)/shard_map/ppermute | solution.py:44
  137.2 9.1 %collective-permute-start.7 = (f32[8,128]{1,0:T(8,128)S(1)}, f32[8,128]{1,0:T(8,128)S(1)}, u32[]{:S(2)}, u32[]{:S(2)}) collective-permute-start(f32[8,128]{1,0:T(8,128)S(1)} %add_add_fusion.1), channel_id=1, source_target_pairs={{0,256},{64,320},{128,384},{192,448},{256,512},{320,576},{384,640}... | collective-permute-start | bytes 12296 | tf_op jit(solution)/shard_map/ppermute | solution.py:44

commit v2 on v1

--- a/solution.py
+++ b/solution.py
@@ -12,23 +12,24 @@
 SWAP = [(0, 1), (1, 0)]
 
 highest = lax.Precision.HIGHEST
+high = lax.Precision.HIGH
 
 
 def rows_dot(a, b):
-    return lax.dot_general(a, b, (((0,), (0,)), ((), ())), precision=highest)
+    return lax.dot_general(a, b, (((0,), (0,)), ((), ())), precision=high)
 
 
 def right_turn(values, basis):
     blocks, order = basis.shape[0], basis.shape[1]
     parts = values.reshape(values.shape[0], blocks, order)
-    out = jnp.einsum("rbc,bcd->rbd", parts, basis, precision=highest)
+    out = jnp.einsum("rbc,bcd->rbd", parts, basis, precision=high)
     return out.reshape(values.shape)
 
 
 def right_back(values, basis):
     blocks, order = basis.shape[0], basis.shape[1]
     parts = values.reshape(values.shape[0], blocks, order)
-    out = jnp.einsum("rbd,bcd->rbc", parts, basis, precision=highest)
+    out = jnp.einsum("rbd,bcd->rbc", parts, basis, precision=high)
     return out.reshape(values.shape)
 
 
@@ -84,17 +85,18 @@
     normal = new_first / (jnp.sqrt(new_second) + 1e-08)
 
     squares = jnp.broadcast_to(jnp.sum(normal * normal), (8, 128))
-    expert_total = shared_total(squares, PLANE_CORE)
-    turned, expert_total = lax.optimization_barrier((right_back(normal, right), expert_total))
-    total = along_z(along_z(expert_total, (1, -1, 2)), (4, -4, 8))[0, 0]
-    count = lax.axis_size("expert") * order * width
-    scale = jnp.sqrt(total / count + 1e-06)
+    near = along_z(squares, (1, -1, 2))
+    turned = right_back(normal, right)
     ours = lax.all_to_all(jnp.broadcast_to(turned, (chips, 2 * rows, width)), PLANE, 0, 0)
     ours = ours.reshape(-1, width)
     theirs = lax.ppermute(ours, "dp_3", SWAP)
-    back = rows_dot(here, ours) + rows_dot(there, theirs)
+    far = along_z(near, (4, -4, 8))
+    total = shared_total(far, PLANE_CORE)[0, 0]
+    count = lax.axis_size("expert") * order * width
+    scale = jnp.sqrt(total / count + 1e-06)
+    back = lax.optimization_barrier(rows_dot(here, ours) + rows_dot(there, theirs))
     own = lambda x: lax.dynamic_slice_in_dim(x, half * rows, rows, 0)
-    return ((back / scale)[None], own(new_first)[None], own(new_second)[None])
+    return ((back * (1.0 / scale))[None], own(new_first)[None], own(new_second)[None])
 
 
 def solution(mesh):

time: 156 us -> 156 us (level)
  starting transfers between devices: 101 us -> 107 us
  matrix products: 17.9 us -> 13.1 us
  waiting for transfers between devices: 23.9 us -> 21.6 us
  other arithmetic: 4.37 us -> 6.6 us
    all_to_all x1, waiting for transfers between devices: 5.56 us -> 0.01 us  [per_device(): lax.all_to_all(jnp.broadcast_to(turned, (chips, 2 * rows, width)), PLANE,...]
    ppermute x6, starting transfers between devices: 22 us -> 27.5 us  [along_z(): lax.ppermute(tile, RING, [(place[z], place[(z + step) % ring]) for z in r...]
    all_to_all x1, starting transfers between devices: 16.1 us -> 10.7 us  [shared_total(): return jnp.sum(lax.all_to_all(tiles, axes, 0, 0), axis=0)]
    dot_general x4, matrix products: 13.1 us -> 8.34 us  [the longest x2 4.57 us: rows_dot(): return lax.dot_general(a, b, (((0,), (0,)), ((), ())), precision=high)]
    ppermute x1, starting transfers between devices: 4.36 us -> 7.79 us  [per_device(): theirs = lax.ppermute(ours, 'dp_3', SWAP)]
    all_to_all x1, waiting for transfers between devices: 4.26 us -> 6.97 us  [shared_total(): return jnp.sum(lax.all_to_all(tiles, axes, 0, 0), axis=0)]
    all_to_all x1, starting transfers between devices: 4.34 us -> 6.15 us  [per_device(): lax.all_to_all(jnp.broadcast_to(turned, (chips, 2 * rows, width)), PLANE,...]
    broadcast_in_dim x1 -> x2, other arithmetic: 0.66 us -> 2.24 us  [the longest x1 1.59 us: per_device(): (back * (1.0 / scale))[None]]
  transfers between devices with their start and end apart: 13 -> 13, of which waited for: 6 -> 5; matrix products, arithmetic and copies ran while one was open for 7% -> 6% of each run, Pallas kernels for 0% -> 0%
where the time goes in v2:
time: 156 us; the launch traced here: 155 us
  starting transfers between devices  107 us (69%)
  waiting for transfers between devices  21.6 us (14%)
  matrix products  13.1 us (8%)
  other arithmetic  6.6 us (4%)
  local copies, waits for them, and re-layouts  4.86 us (3%)
  between operations  1.65 us (1%)
    ppermute x6, starting transfers between devices, along_z(): lax.ppermute(tile, RING, [(place[z], place[(z + step) % ring]) for z in r...  27.5 us
    ppermute x1, starting transfers between devices, per_device(): moments_there = lax.ppermute(moments, 'dp_2', SWAP)  18.5 us
    ppermute x1, starting transfers between devices, per_device(): pair = kept + lax.ppermute(sent, 'dp_3', SWAP)  16 us
    ppermute x1, starting transfers between devices, per_device(): summed = partial + lax.ppermute(partial, 'dp_2', SWAP)  15.8 us
    all_to_all x1, starting transfers between devices, shared_total(): return jnp.sum(lax.all_to_all(tiles, axes, 0, 0), axis=0)  10.7 us
    ppermute x1, waiting for transfers between devices, per_device(): summed = partial + lax.ppermute(partial, 'dp_2', SWAP)  8.18 us
    ppermute x1, starting transfers between devices, per_device(): theirs = lax.ppermute(ours, 'dp_3', SWAP)  7.79 us
    all_to_all x1, waiting for transfers between devices, shared_total(): return jnp.sum(lax.all_to_all(tiles, axes, 0, 0), axis=0)  6.97 us
  transfers between devices with their start and end apart: 13, of which 5 were waited for; matrix products, arithmetic and copies ran while one was open for 6% of the time, Pallas kernels for 0%

profile of v2, /device:TPU:1, one launch (start us, length us, event | category | flops | bytes accessed | tf_op | source)
XLA Modules:
  0.0 154.7 jit_solution(17066326153570584578)
XLA Ops:
  0.7 1.7 %copy.13 = f32[1,512,512]{1,2,0:T(8,128)S(1)} copy(f32[1,512,512]{2,1,0:T(8,128)} %param.8) | data formatting | bytes 2097152 | tf_op args[3]
  2.5 2.9 %fusion.4 = f32[256,1024]{1,0:T(8,128)} fusion(f32[1,1,512,1024]{3,2,1,0:T(8,128)S(1)} %copy-done, f32[32,2,8,512]{3,2,1,0:T(8,128)S(1)} %bitcast.73, s32[]{:T(128)S(6)} %select_n.35), kind=kOutput, calls=%fused_computation.4 | convolution fusion | flops 1610612736 | bytes 3670020 | tf_op jit(solution)/shard_map/dot_general | solution.py:70
  5.4 16.0 %collective-permute-start.1 = (f32[256,1024]{1,0:T(8,128)}, f32[256,1024]{1,0:T(8,128)}, u32[]{:S(2)}, u32[]{:S(2)}) collective-permute-start(f32[256,1024]{1,0:T(8,128)} %fusion.4), channel_id=1, source_target_pairs={{0,1},{1,0},{2,3},{3,2},{4,5},{5,4},{6,7},{7,6},{8,9},{9,8},{10,11... | collective-permute-start | bytes 3145736 | tf_op jit(solution)/shard_map/ppermute | solution.py:72
  21.4 1.9 %fusion.6 = f32[256,1024]{1,0:T(8,128)S(1)} fusion(f32[1,1,512,1024]{3,2,1,0:T(8,128)S(1)} %copy-done, f32[32,2,8,512]{3,2,1,0:T(8,128)S(1)} %bitcast.74, s32[]{:T(128)S(6)} %select_n.31), kind=kOutput, calls=%fused_computation.6 | convolution fusion | flops 1610612736 | bytes 3670020 | tf_op jit(solution)/shard_map/dot_general | solution.py:71
  24.0 2.3 %add.67 = f32[256,1024]{1,0:T(8,128)} add(f32[256,1024]{1,0:T(8,128)S(1)} %fusion.6, f32[256,1024]{1,0:T(8,128)} %collective-permute-done.1) | non-fusion elementwise | flops 262144 | bytes 3145728 | tf_op jit(solution)/shard_map/add | solution.py:72
  26.4 4.3 %all-to-all-start = ((f32[16,16,1024]{2,1,0:T(8,128)}), f32[16,16,1024]{2,1,0:T(8,128)}, u32[]{:S(2)}, u32[]{:S(2)}) async-start(f32[16,16,1024]{2,1,0:T(8,128)} %bitcast.77), calls=%async_computation | async-start | bytes 2097152 | tf_op jit(solution)/shard_map/all_to_all | solution.py:73
  30.7 18.5 %collective-permute-start = (f32[16,1024]{1,0:T(8,128)S(1)}, f32[16,1024]{1,0:T(8,128)S(1)}, u32[]{:S(2)}, u32[]{:S(2)}) collective-permute-start(f32[16,1024]{1,0:T(8,128)S(1)} %pad_maximum_fusion), channel_id=1, source_target_pairs={{0,2},{2,0},{1,3},{3,1},{4,6},{6,4},{5,7},{7,5},{8,10},{10,8},{9,1... | collective-permute-start | bytes 196616 | tf_op jit(solution)/shard_map/ppermute | solution.py:77
  50.6 15.8 %collective-permute-start.2 = (f32[16,1024]{1,0:T(8,128)S(1)}, f32[16,1024]{1,0:T(8,128)S(1)}, u32[]{:S(2)}, u32[]{:S(2)}) collective-permute-start(f32[16,1024]{1,0:T(8,128)S(1)} %reduce_sum.27), channel_id=1, source_target_pairs={{0,2},{2,0},{1,3},{3,1},{4,6},{6,4},{5,7},{7,5},{8,10},{10,8},{9,1... | collective-permute-start | bytes 196616 | tf_op jit(solution)/shard_map/ppermute | solution.py:81
  66.4 8.2 %collective-permute-done.2 = f32[16,1024]{1,0:T(8,128)S(1)} collective-permute-done((f32[16,1024]{1,0:T(8,128)S(1)}, f32[16,1024]{1,0:T(8,128)S(1)}, u32[]{:S(2)}, u32[]{:S(2)}) %collective-permute-start.2) | collective-permute-done | bytes 65568 | tf_op jit(solution)/shard_map/ppermute | solution.py:81
  74.6 2.8 %multiply_reduce_fusion = (f32[]{:T(128)}, f32[16,2,512]{2,0,1:T(8,128)S(1)}, f32[2,16,512]{2,1,0:T(8,128)S(1)}) fusion(f32[8,2,512]{2,0,1:T(8,128)S(1)} %bitcast.80, f32[8,2,512]{2,0,1:T(8,128)S(1)} %bitcast.81, f32[8,2,512]{2,0,1:T(8,128)S(1)} %bitcast.79, f32[8,2,512]{2,0,1:T(8,128)S(1)} %bitcast.78, f32[1,2,512,512]{3,2,1,0:T(8,128)} %param.9, ...), kind=kOutput, calls=%fused_computation.34 | convolution fusion | flops 50561024 | bytes 2424836 | tf_op jit(solution)/shard_map/rbc,bcd->rbd/dot_general | solution.py:25
  79.5 6.1 %all-to-all-start.1 = ((f32[16,16,1024]{2,1,0:T(8,128)}), f32[16,16,1024]{2,1,0:T(8,128)}, u32[]{:S(2)}, u32[]{:S(2)}) async-start(f32[16,16,1024]{2,1,0:T(8,128)} %broadcast_in_dim.18), calls=%async_computation.1 | async-start | bytes 2097152 | tf_op jit(solution)/shard_map/all_to_all | solution.py:90
  86.3 12.3 %collective-permute-start.5 = (f32[8,128]{1,0:T(8,128)S(1)}, f32[8,128]{1,0:T(8,128)S(1)}, u32[]{:S(2)}, u32[]{:S(2)}) collective-permute-start(f32[8,128]{1,0:T(8,128)S(1)} %broadcast_in_dim.19), channel_id=1, source_target_pairs={{0,962},{64,0},{128,64},{192,128},{256,192},{320,256},{384,320},{4... | collective-permute-start | bytes 12296 | tf_op jit(solution)/shard_map/ppermute | solution.py:45
  98.6 1.9 %collective-permute-start.6 = (f32[8,128]{1,0:T(8,128)S(1)}, f32[8,128]{1,0:T(8,128)S(1)}, u32[]{:S(2)}, u32[]{:S(2)}) collective-permute-start(f32[8,128]{1,0:T(8,128)S(1)} %broadcast_in_dim.19), channel_id=1, source_target_pairs={{0,128},{64,192},{128,256},{192,320},{256,384},{320,448},{384,512}... | collective-permute-start | bytes 12296 | tf_op jit(solution)/shard_map/ppermute | solution.py:45
  100.6 1.9 %collective-permute-start.4 = (f32[8,128]{1,0:T(8,128)S(1)}, f32[8,128]{1,0:T(8,128)S(1)}, u32[]{:S(2)}, u32[]{:S(2)}) collective-permute-start(f32[8,128]{1,0:T(8,128)S(1)} %broadcast_in_dim.19), channel_id=1, source_target_pairs={{0,64},{64,128},{128,192},{192,256},{256,320},{320,384},{384,448},... | collective-permute-start | bytes 12296 | tf_op jit(solution)/shard_map/ppermute | solution.py:45
  102.5 7.8 %collective-permute-start.3 = (f32[256,1024]{1,0:T(8,128)}, f32[256,1024]{1,0:T(8,128)}, u32[]{:S(2)}, u32[]{:S(2)}) collective-permute-start(f32[256,1024]{1,0:T(8,128)} %bitcast.19), channel_id=1, source_target_pairs={{0,1},{1,0},{2,3},{3,2},{4,5},{5,4},{6,7},{7,6},{8,9},{9,8},{10,11... | collective-permute-start | bytes 3145736 | tf_op jit(solution)/shard_map/ppermute | solution.py:92
  111.0 1.9 %collective-permute-start.9 = (f32[8,128]{1,0:T(8,128)S(1)}, f32[8,128]{1,0:T(8,128)S(1)}, u32[]{:S(2)}, u32[]{:S(2)}) collective-permute-start(f32[8,128]{1,0:T(8,128)S(1)} %add_add_fusion.1), channel_id=1, source_target_pairs={{0,512},{64,576},{128,640},{192,704},{256,768},{320,832},{384,896}... | collective-permute-start | bytes 12296 | tf_op jit(solution)/shard_map/ppermute | solution.py:45
  112.9 6.2 %collective-permute-start.8 = (f32[8,128]{1,0:T(8,128)S(1)}, f32[8,128]{1,0:T(8,128)S(1)}, u32[]{:S(2)}, u32[]{:S(2)}) collective-permute-start(f32[8,128]{1,0:T(8,128)S(1)} %add_add_fusion.1), channel_id=1, source_target_pairs={{0,770},{64,834},{128,898},{192,962},{256,0},{320,64},{384,128},{4... | collective-permute-start | bytes 12296 | tf_op jit(solution)/shard_map/ppermute | solution.py:45
  119.2 3.2 %collective-permute-start.7 = (f32[8,128]{1,0:T(8,128)S(1)}, f32[8,128]{1,0:T(8,128)S(1)}, u32[]{:S(2)}, u32[]{:S(2)}) collective-permute-start(f32[8,128]{1,0:T(8,128)S(1)} %add_add_fusion.1), channel_id=1, source_target_pairs={{0,256},{64,320},{128,384},{192,448},{256,512},{320,576},{384,640}... | collective-permute-start | bytes 12296 | tf_op jit(solution)/shard_map/ppermute | solution.py:45
  122.4 1.7 %collective-permute-done.9 = f32[8,128]{1,0:T(8,128)S(1)} collective-permute-done((f32[8,128]{1,0:T(8,128)S(1)}, f32[8,128]{1,0:T(8,128)S(1)}, u32[]{:S(2)}, u32[]{:S(2)}) %collective-permute-start.9) | collective-permute-done | bytes 4128 | tf_op jit(solution)/shard_map/ppermute | solution.py:45
  124.1 4.1 %collective-permute-done.7 = f32[8,128]{1,0:T(8,128)S(1)} collective-permute-done((f32[8,128]{1,0:T(8,128)S(1)}, f32[8,128]{1,0:T(8,128)S(1)}, u32[]{:S(2)}, u32[]{:S(2)}) %collective-permute-start.7) | collective-permute-done | bytes 4128 | tf_op jit(solution)/shard_map/ppermute | solution.py:45
  128.9 10.7 %all-to-all-start.2 = ((f32[32,8,128]{2,1,0:T(8,128)}), f32[32,8,128]{2,1,0:T(8,128)S(1)}, u32[]{:S(2)}, u32[]{:S(2)}) async-start(f32[32,8,128]{2,1,0:T(8,128)} %broadcast_in_dim.20), calls=%async_computation.2 | async-start | bytes 262144 | tf_op jit(solution)/shard_map/all_to_all | solution.py:38
  140.3 7.0 %all-to-all-done.2 = f32[32,8,128]{2,1,0:T(8,128)S(1)} async-done(((f32[32,8,128]{2,1,0:T(8,128)}), f32[32,8,128]{2,1,0:T(8,128)S(1)}, u32[]{:S(2)}, u32[]{:S(2)}) %all-to-all-start.2) | async-done | bytes 131104 | tf_op jit(solution)/shard_map/all_to_all | solution.py:38
  148.5 2.3 %fusion.13 = f32[512,1024]{1,0:T(8,128)S(1)} fusion(f32[256,1024]{1,0:T(8,128)} %bitcast.19, f32[32,2,8,512]{3,2,1,0:T(8,128)S(1)} %bitcast.75, s32[]{:T(128)S(6)} %select_n.31), kind=kOutput, calls=%fused_computation.13 | convolution fusion | flops 805306368 | bytes 3670020 | tf_op jit(solution)/shard_map/dot_general | solution.py:19
  150.8 2.3 %convolution_add_fusion = f32[512,1024]{1,0:T(8,128)S(1)} fusion(f32[512,1024]{1,0:T(8,128)S(1)} %fusion.13, f32[256,1024]{1,0:T(8,128)} %collective-permute-done.3, f32[32,2,8,512]{3,2,1,0:T(8,128)S(1)} %bitcast.76, s32[]{:T(128)S(6)} %select_n.35), kind=kOutput, calls=%fused_computation.9 | convolution fusion | flops 805830656 | bytes 5767172 | tf_op jit(solution)/shard_map/dot_general | solution.py:19
  (35 shorter events, 9.0 us)
Async XLA Ops:
  0.6 1.9 %copy-start = (f32[1,1,512,1024]{3,2,1,0:T(8,128)S(1)}, f32[1,1,512,1024]{3,2,1,0:T(8,128)}, u32[]{:S(2)}) copy-start(f32[1,1,512,1024]{3,2,1,0:T(8,128)} %param.5) | copy-start | bytes 6291460
  5.4 18.6 %collective-permute-start.1 = (f32[256,1024]{1,0:T(8,128)}, f32[256,1024]{1,0:T(8,128)}, u32[]{:S(2)}, u32[]{:S(2)}) collective-permute-start(f32[256,1024]{1,0:T(8,128)} %fusion.4), channel_id=1, source_target_pairs={{0,1},{1,0},{2,3},{3,2},{4,5},{5,4},{6,7},{7,6},{8,9},{9,8},{10,11... | collective-permute-start | bytes 3145736 | tf_op jit(solution)/shard_map/ppermute | solution.py:72
  23.3 7.4 %copy-start.2 = (f32[1,8,1024]{2,1,0:T(8,128)S(1)}, f32[1,8,1024]{2,1,0:T(8,128)}, u32[]{:S(2)}) copy-start(f32[1,8,1024]{2,1,0:T(8,128)} %param.7) | copy-start | bytes 98308
  23.3 7.4 %copy-start.3 = (f32[1,8,1024]{2,1,0:T(8,128)S(1)}, f32[1,8,1024]{2,1,0:T(8,128)}, u32[]{:S(2)}) copy-start(f32[1,8,1024]{2,1,0:T(8,128)} %param.6) | copy-start | bytes 98308
  26.4 22.9 %all-to-all-start = ((f32[16,16,1024]{2,1,0:T(8,128)}), f32[16,16,1024]{2,1,0:T(8,128)}, u32[]{:S(2)}, u32[]{:S(2)}) async-start(f32[16,16,1024]{2,1,0:T(8,128)} %bitcast.77), calls=%async_computation | async-start | bytes 2097152 | tf_op jit(solution)/shard_map/all_to_all | solution.py:73
  30.7 35.7 %collective-permute-start = (f32[16,1024]{1,0:T(8,128)S(1)}, f32[16,1024]{1,0:T(8,128)S(1)}, u32[]{:S(2)}, u32[]{:S(2)}) collective-permute-start(f32[16,1024]{1,0:T(8,128)S(1)} %pad_maximum_fusion), channel_id=1, source_target_pairs={{0,2},{2,0},{1,3},{3,1},{4,6},{6,4},{5,7},{7,5},{8,10},{10,8},{9,1... | collective-permute-start | bytes 196616 | tf_op jit(solution)/shard_map/ppermute | solution.py:77
  50.6 26.9 %copy-start.1 = (f32[1,2,512,512]{3,2,1,0:T(8,128)S(1)}, f32[1,2,512,512]{3,2,1,0:T(8,128)}, u32[]{:S(2)}) copy-start(f32[1,2,512,512]{3,2,1,0:T(8,128)} %param.9) | copy-start | bytes 6291460
  50.6 24.0 %collective-permute-start.2 = (f32[16,1024]{1,0:T(8,128)S(1)}, f32[16,1024]{1,0:T(8,128)S(1)}, u32[]{:S(2)}, u32[]{:S(2)}) collective-permute-start(f32[16,1024]{1,0:T(8,128)S(1)} %reduce_sum.27), channel_id=1, source_target_pairs={{0,2},{2,0},{1,3},{3,1},{4,6},{6,4},{5,7},{7,5},{8,10},{10,8},{9,1... | collective-permute-start | bytes 196616 | tf_op jit(solution)/shard_map/ppermute | solution.py:81
  79.5 23.0 %all-to-all-start.1 = ((f32[16,16,1024]{2,1,0:T(8,128)}), f32[16,16,1024]{2,1,0:T(8,128)}, u32[]{:S(2)}, u32[]{:S(2)}) async-start(f32[16,16,1024]{2,1,0:T(8,128)} %broadcast_in_dim.18), calls=%async_computation.1 | async-start | bytes 2097152 | tf_op jit(solution)/shard_map/all_to_all | solution.py:90
  86.3 24.0 %collective-permute-start.5 = (f32[8,128]{1,0:T(8,128)S(1)}, f32[8,128]{1,0:T(8,128)S(1)}, u32[]{:S(2)}, u32[]{:S(2)}) collective-permute-start(f32[8,128]{1,0:T(8,128)S(1)} %broadcast_in_dim.19), channel_id=1, source_target_pairs={{0,962},{64,0},{128,64},{192,128},{256,192},{320,256},{384,320},{4... | collective-permute-start | bytes 12296 | tf_op jit(solution)/shard_map/ppermute | solution.py:45
  98.6 11.7 %collective-permute-start.6 = (f32[8,128]{1,0:T(8,128)S(1)}, f32[8,128]{1,0:T(8,128)S(1)}, u32[]{:S(2)}, u32[]{:S(2)}) collective-permute-start(f32[8,128]{1,0:T(8,128)S(1)} %broadcast_in_dim.19), channel_id=1, source_target_pairs={{0,128},{64,192},{128,256},{192,320},{256,384},{320,448},{384,512}... | collective-permute-start | bytes 12296 | tf_op jit(solution)/shard_map/ppermute | solution.py:45
  100.6 9.8 %collective-permute-start.4 = (f32[8,128]{1,0:T(8,128)S(1)}, f32[8,128]{1,0:T(8,128)S(1)}, u32[]{:S(2)}, u32[]{:S(2)}) collective-permute-start(f32[8,128]{1,0:T(8,128)S(1)} %broadcast_in_dim.19), channel_id=1, source_target_pairs={{0,64},{64,128},{128,192},{192,256},{256,320},{320,384},{384,448},... | collective-permute-start | bytes 12296 | tf_op jit(solution)/shard_map/ppermute | solution.py:45
  102.5 48.3 %collective-permute-start.3 = (f32[256,1024]{1,0:T(8,128)}, f32[256,1024]{1,0:T(8,128)}, u32[]{:S(2)}, u32[]{:S(2)}) collective-permute-start(f32[256,1024]{1,0:T(8,128)} %bitcast.19), channel_id=1, source_target_pairs={{0,1},{1,0},{2,3},{3,2},{4,5},{5,4},{6,7},{7,6},{8,9},{9,8},{10,11... | collective-permute-start | bytes 3145736 | tf_op jit(solution)/shard_map/ppermute | solution.py:92
  111.0 13.1 %collective-permute-start.9 = (f32[8,128]{1,0:T(8,128)S(1)}, f32[8,128]{1,0:T(8,128)S(1)}, u32[]{:S(2)}, u32[]{:S(2)}) collective-permute-start(f32[8,128]{1,0:T(8,128)S(1)} %add_add_fusion.1), channel_id=1, source_target_pairs={{0,512},{64,576},{128,640},{192,704},{256,768},{320,832},{384,896}... | collective-permute-start | bytes 12296 | tf_op jit(solution)/shard_map/ppermute | solution.py:45
  112.9 11.1 %collective-permute-start.8 = (f32[8,128]{1,0:T(8,128)S(1)}, f32[8,128]{1,0:T(8,128)S(1)}, u32[]{:S(2)}, u32[]{:S(2)}) collective-permute-start(f32[8,128]{1,0:T(8,128)S(1)} %add_add_fusion.1), channel_id=1, source_target_pairs={{0,770},{64,834},{128,898},{192,962},{256,0},{320,64},{384,128},{4... | collective-permute-start | bytes 12296 | tf_op jit(solution)/shard_map/ppermute | solution.py:45
  119.2 9.0 %collective-permute-start.7 = (f32[8,128]{1,0:T(8,128)S(1)}, f32[8,128]{1,0:T(8,128)S(1)}, u32[]{:S(2)}, u32[]{:S(2)}) collective-permute-start(f32[8,128]{1,0:T(8,128)S(1)} %add_add_fusion.1), channel_id=1, source_target_pairs={{0,256},{64,320},{128,384},{192,448},{256,512},{320,576},{384,640}... | collective-permute-start | bytes 12296 | tf_op jit(solution)/shard_map/ppermute | solution.py:45
  128.9 18.4 %all-to-all-start.2 = ((f32[32,8,128]{2,1,0:T(8,128)}), f32[32,8,128]{2,1,0:T(8,128)S(1)}, u32[]{:S(2)}, u32[]{:S(2)}) async-start(f32[32,8,128]{2,1,0:T(8,128)} %broadcast_in_dim.20), calls=%async_computation.2 | async-start | bytes 262144 | tf_op jit(solution)/shard_map/all_to_all | solution.py:38

commit v3 on v2

--- a/solution.py
+++ b/solution.py
@@ -8,7 +8,7 @@
 DP = ("dp_0", "dp_1", "dp_2", "dp_3")
 PLANE = ("dp_0", "dp_1")
 PLANE_CORE = ("dp_0", "dp_1", "dp_3")
-RING = ("expert", "dp_2")
+CHIPS = ("expert", "dp_0", "dp_1", "dp_2")
 SWAP = [(0, 1), (1, 0)]
 
 highest = lax.Precision.HIGHEST
@@ -38,14 +38,20 @@
     return jnp.sum(lax.all_to_all(tiles, axes, 0, 0), axis=0)
 
 
-def along_z(tile, steps):
-    ring, experts = lax.axis_size(RING), lax.axis_size("expert")
-    place = [z % experts * (ring // experts) + z // experts for z in range(ring)]
-    moved = [
-        lax.ppermute(tile, RING, [(place[z], place[(z + step) % ring]) for z in range(ring)])
-        for step in steps
+def along_z(tile):
+    experts, split_x, split_y, split_z = (lax.axis_size(axis) for axis in CHIPS)
+    ring = experts * split_z
+
+    def index(place, p):
+        e, z = place % experts, place // experts
+        return (e * split_x * split_y + p) * split_z + z
+
+    pairs = [
+        (index(place, p), index((place + p - experts // 2) % ring, p))
+        for place in range(ring)
+        for p in range(split_x * split_y)
     ]
-    return sum(moved, tile)
+    return lax.ppermute(tile, CHIPS, pairs)
 
 
 def halves(own, other, index):
@@ -85,16 +91,17 @@
     normal = new_first / (jnp.sqrt(new_second) + 1e-08)
 
     squares = jnp.broadcast_to(jnp.sum(normal * normal), (8, 128))
-    near = along_z(squares, (1, -1, 2))
+    expert_sum = shared_total(squares, PLANE_CORE)
     turned = right_back(normal, right)
     ours = lax.all_to_all(jnp.broadcast_to(turned, (chips, 2 * rows, width)), PLANE, 0, 0)
     ours = ours.reshape(-1, width)
     theirs = lax.ppermute(ours, "dp_3", SWAP)
-    far = along_z(near, (4, -4, 8))
-    total = shared_total(far, PLANE_CORE)[0, 0]
+    another = along_z(expert_sum)
+    total = shared_total(another, PLANE)[0, 0]
     count = lax.axis_size("expert") * order * width
     scale = jnp.sqrt(total / count + 1e-06)
-    back = lax.optimization_barrier(rows_dot(here, ours) + rows_dot(there, theirs))
+    back = rows_dot(here, ours)
+    back = back + rows_dot(there, theirs)
     own = lambda x: lax.dynamic_slice_in_dim(x, half * rows, rows, 0)
     return ((back * (1.0 / scale))[None], own(new_first)[None], own(new_second)[None])
 

time: 156 us -> 156 us (level); the launches traced: 155 us -> 153 us
  starting transfers between devices: 107 us -> 79.5 us
  blocking collectives: 0 us -> 17.8 us
  waiting for transfers between devices: 21.6 us -> 30.5 us
  other arithmetic: 6.6 us -> 4.37 us
    ppermute x6 -> x1, starting transfers between devices: 27.5 us -> 4.81 us  [along_z(): return lax.ppermute(tile, CHIPS, pairs)]
    all_to_all x0 -> x1, blocking collectives: none -> 17.8 us  [per_device(): lax.all_to_all(jnp.broadcast_to(turned, (chips, 2 * rows, width)), PLANE,...]
    all_to_all x1 -> x2, waiting for transfers between devices: 6.97 us -> 13.5 us  [shared_total(): return jnp.sum(lax.all_to_all(tiles, axes, 0, 0), axis=0)]
    all_to_all x1 -> x0, starting transfers between devices: 6.15 us -> none  [per_device(): lax.all_to_all(jnp.broadcast_to(turned, (chips, 2 * rows, width)), PLANE,...]
    ppermute x1, starting transfers between devices: 7.79 us -> 12.8 us  [per_device(): theirs = lax.ppermute(ours, 'dp_3', SWAP)]
    all_to_all x1 -> x2, starting transfers between devices: 10.7 us -> 7.15 us  [shared_total(): return jnp.sum(lax.all_to_all(tiles, axes, 0, 0), axis=0)]
    ppermute x6 -> x1, waiting for transfers between devices: 5.79 us -> 8.19 us  [along_z(): return lax.ppermute(tile, CHIPS, pairs)]
    broadcast_in_dim x1 -> x0, other arithmetic: 1.59 us -> none  [per_device(): (back * (1.0 / scale))[None]]
  transfers between devices with their start and end apart: 13 -> 8, of which waited for: 5 -> 5; matrix products, arithmetic and copies ran while one was open for 6% -> 6% of each run, Pallas kernels for 0% -> 0%
where the time goes in v3:
time: 156 us; the launch traced here: 153 us
  starting transfers between devices  79.5 us (51%)
  waiting for transfers between devices  30.5 us (20%)
  blocking collectives  17.8 us (11%)
  matrix products  14.5 us (9%)
  local copies, waits for them, and re-layouts  4.51 us (3%)
  other arithmetic  4.37 us (3%)
  between operations  1.56 us (1%)
    ppermute x1, starting transfers between devices, per_device(): moments_there = lax.ppermute(moments, 'dp_2', SWAP)  18.5 us
    all_to_all x1, blocking collectives, per_device(): lax.all_to_all(jnp.broadcast_to(turned, (chips, 2 * rows, width)), PLANE,...  17.8 us
    ppermute x1, starting transfers between devices, per_device(): pair = kept + lax.ppermute(sent, 'dp_3', SWAP)  16 us
    ppermute x1, starting transfers between devices, per_device(): summed = partial + lax.ppermute(partial, 'dp_2', SWAP)  15.8 us
    all_to_all x2, waiting for transfers between devices, shared_total(): return jnp.sum(lax.all_to_all(tiles, axes, 0, 0), axis=0)  13.5 us
    ppermute x1, starting transfers between devices, per_device(): theirs = lax.ppermute(ours, 'dp_3', SWAP)  12.8 us
    ppermute x1, waiting for transfers between devices, along_z(): return lax.ppermute(tile, CHIPS, pairs)  8.19 us
    ppermute x1, waiting for transfers between devices, per_device(): summed = partial + lax.ppermute(partial, 'dp_2', SWAP)  8.18 us
  transfers between devices with their start and end apart: 8, of which 5 were waited for; matrix products, arithmetic and copies ran while one was open for 6% of the time, Pallas kernels for 0%

profile of v3, /device:TPU:1, one launch (start us, length us, event | category | flops | bytes accessed | tf_op | source)
XLA Modules:
  0.0 152.7 jit_solution(6192149255997680303)
XLA Ops:
  0.7 1.7 %copy.13 = f32[1,512,512]{1,2,0:T(8,128)S(1)} copy(f32[1,512,512]{2,1,0:T(8,128)} %param.8) | data formatting | bytes 2097152 | tf_op args[3]
  2.5 2.9 %fusion.4 = f32[256,1024]{1,0:T(8,128)} fusion(f32[1,1,512,1024]{3,2,1,0:T(8,128)S(1)} %copy-done, f32[32,2,8,512]{3,2,1,0:T(8,128)S(1)} %bitcast.73, s32[]{:T(128)S(6)} %select_n.35), kind=kOutput, calls=%fused_computation.4 | convolution fusion | flops 1610612736 | bytes 3670020 | tf_op jit(solution)/shard_map/dot_general | solution.py:76
  5.4 16.0 %collective-permute-start.1 = (f32[256,1024]{1,0:T(8,128)}, f32[256,1024]{1,0:T(8,128)}, u32[]{:S(2)}, u32[]{:S(2)}) collective-permute-start(f32[256,1024]{1,0:T(8,128)} %fusion.4), channel_id=1, source_target_pairs={{0,1},{1,0},{2,3},{3,2},{4,5},{5,4},{6,7},{7,6},{8,9},{9,8},{10,11... | collective-permute-start | bytes 3145736 | tf_op jit(solution)/shard_map/ppermute | solution.py:78
  21.4 1.9 %fusion.6 = f32[256,1024]{1,0:T(8,128)S(1)} fusion(f32[1,1,512,1024]{3,2,1,0:T(8,128)S(1)} %copy-done, f32[32,2,8,512]{3,2,1,0:T(8,128)S(1)} %bitcast.74, s32[]{:T(128)S(6)} %select_n.31), kind=kOutput, calls=%fused_computation.6 | convolution fusion | flops 1610612736 | bytes 3670020 | tf_op jit(solution)/shard_map/dot_general | solution.py:77
  23.4 0.7 collective-permute-done.1
  24.0 2.3 %add.49 = f32[256,1024]{1,0:T(8,128)} add(f32[256,1024]{1,0:T(8,128)S(1)} %fusion.6, f32[256,1024]{1,0:T(8,128)} %collective-permute-done.1) | non-fusion elementwise | flops 262144 | bytes 3145728 | tf_op jit(solution)/shard_map/add | solution.py:78
  26.4 4.3 %all-to-all-start = ((f32[16,16,1024]{2,1,0:T(8,128)}), f32[16,16,1024]{2,1,0:T(8,128)}, u32[]{:S(2)}, u32[]{:S(2)}) async-start(f32[16,16,1024]{2,1,0:T(8,128)} %bitcast.77), calls=%async_computation | async-start | bytes 2097152 | tf_op jit(solution)/shard_map/all_to_all | solution.py:79
  30.7 18.5 %collective-permute-start = (f32[16,1024]{1,0:T(8,128)S(1)}, f32[16,1024]{1,0:T(8,128)S(1)}, u32[]{:S(2)}, u32[]{:S(2)}) collective-permute-start(f32[16,1024]{1,0:T(8,128)S(1)} %pad_maximum_fusion), channel_id=1, source_target_pairs={{0,2},{2,0},{1,3},{3,1},{4,6},{6,4},{5,7},{7,5},{8,10},{10,8},{9,1... | collective-permute-start | bytes 196616 | tf_op jit(solution)/shard_map/ppermute | solution.py:83
  49.3 1.3 reduce_sum.36
  50.6 15.8 %collective-permute-start.2 = (f32[16,1024]{1,0:T(8,128)S(1)}, f32[16,1024]{1,0:T(8,128)S(1)}, u32[]{:S(2)}, u32[]{:S(2)}) collective-permute-start(f32[16,1024]{1,0:T(8,128)S(1)} %reduce_sum.36), channel_id=1, source_target_pairs={{0,2},{2,0},{1,3},{3,1},{4,6},{6,4},{5,7},{7,5},{8,10},{10,8},{9,1... | collective-permute-start | bytes 196616 | tf_op jit(solution)/shard_map/ppermute | solution.py:87
  66.4 8.2 %collective-permute-done.2 = f32[16,1024]{1,0:T(8,128)S(1)} collective-permute-done((f32[16,1024]{1,0:T(8,128)S(1)}, f32[16,1024]{1,0:T(8,128)S(1)}, u32[]{:S(2)}, u32[]{:S(2)}) %collective-permute-start.2) | collective-permute-done | bytes 65568 | tf_op jit(solution)/shard_map/ppermute | solution.py:87
  74.6 2.8 %multiply_reduce_fusion = (f32[]{:T(128)}, f32[16,2,512]{2,0,1:T(8,128)S(1)}, f32[2,16,512]{2,1,0:T(8,128)S(1)}) fusion(f32[8,2,512]{2,0,1:T(8,128)S(1)} %bitcast.80, f32[8,2,512]{2,0,1:T(8,128)S(1)} %bitcast.81, f32[8,2,512]{2,0,1:T(8,128)S(1)} %bitcast.79, f32[8,2,512]{2,0,1:T(8,128)S(1)} %bitcast.78, f32[1,2,512,512]{3,2,1,0:T(8,128)} %param.9, ...), kind=kOutput, calls=%fused_computation.33 | convolution fusion | flops 50561024 | bytes 2424836 | tf_op jit(solution)/shard_map/rbc,bcd->rbd/dot_general | solution.py:25
  77.5 0.9 fusion.8
  78.5 17.8 %all_to_all.20 = f32[16,16,1024]{2,1,0:T(8,128)} all-to-all(f32[16,16,1024]{2,1,0:T(8,128)S(1)} %broadcast_in_dim.15), channel_id=1, replica_groups=mesh['expert'=16,'dp_0'=4,'dp_1'=4,'dp_2'=2,'dp_3'=2] {'dp_0','dp_1'}, dimensions={0} | all-to-all | bytes 2097152 | tf_op jit(solution)/shard_map/all_to_all | solution.py:96
  96.3 12.8 %collective-permute-start.3 = (f32[256,1024]{1,0:T(8,128)}, f32[256,1024]{1,0:T(8,128)}, u32[]{:S(2)}, u32[]{:S(2)}) collective-permute-start(f32[256,1024]{1,0:T(8,128)} %bitcast.19), channel_id=1, source_target_pairs={{0,1},{1,0},{2,3},{3,2},{4,5},{5,4},{6,7},{7,6},{8,9},{9,8},{10,11... | collective-permute-start | bytes 3145736 | tf_op jit(solution)/shard_map/ppermute | solution.py:98
  109.1 1.3 broadcast_in_dim_broadcast_in_dim.3
  110.4 3.6 %all-to-all-start.2 = ((f32[32,8,128]{2,1,0:T(8,128)}), f32[32,8,128]{2,1,0:T(8,128)S(1)}, u32[]{:S(2)}, u32[]{:S(2)}) async-start(f32[32,8,128]{2,1,0:T(8,128)} %broadcast_in_dim_broadcast_in_dim.3), calls=%async_computation.2 | async-start | bytes 262144 | tf_op jit(solution)/shard_map/all_to_all | solution.py:38
  114.1 7.7 %all-to-all-done.2 = f32[32,8,128]{2,1,0:T(8,128)S(1)} async-done(((f32[32,8,128]{2,1,0:T(8,128)}), f32[32,8,128]{2,1,0:T(8,128)S(1)}, u32[]{:S(2)}, u32[]{:S(2)}) %all-to-all-start.2) | async-done | bytes 131104 | tf_op jit(solution)/shard_map/all_to_all | solution.py:38
  121.8 4.8 %collective-permute-start.4 = (f32[8,128]{1,0:T(8,128)S(1)}, f32[8,128]{1,0:T(8,128)S(1)}, u32[]{:S(2)}, u32[]{:S(2)}) collective-permute-start(f32[8,128]{1,0:T(8,128)S(1)} %reduce_sum.38), channel_id=1, source_target_pairs={{0,514},{4,582},{8,650},{12,718},{16,786},{20,854},{24,922},{28,99... | collective-permute-start | bytes 12296 | tf_op jit(solution)/shard_map/ppermute | solution.py:54
  126.7 8.2 %collective-permute-done.4 = f32[8,128]{1,0:T(8,128)S(1)} collective-permute-done((f32[8,128]{1,0:T(8,128)S(1)}, f32[8,128]{1,0:T(8,128)S(1)}, u32[]{:S(2)}, u32[]{:S(2)}) %collective-permute-start.4) | collective-permute-done | bytes 4128 | tf_op jit(solution)/shard_map/ppermute | solution.py:54
  135.5 3.5 %all-to-all-start.3 = ((f32[16,8,128]{2,1,0:T(8,128)}), f32[16,8,128]{2,1,0:T(8,128)S(1)}, u32[]{:S(2)}, u32[]{:S(2)}) async-start(f32[16,8,128]{2,1,0:T(8,128)} %broadcast_in_dim.16), calls=%async_computation.3 | async-start | bytes 131072 | tf_op jit(solution)/shard_map/all_to_all | solution.py:38
  139.7 5.8 %all-to-all-done.3 = f32[16,8,128]{2,1,0:T(8,128)S(1)} async-done(((f32[16,8,128]{2,1,0:T(8,128)}), f32[16,8,128]{2,1,0:T(8,128)S(1)}, u32[]{:S(2)}, u32[]{:S(2)}) %all-to-all-start.3) | async-done | bytes 65568 | tf_op jit(solution)/shard_map/all_to_all | solution.py:38
  146.7 2.3 %fusion.13 = f32[512,1024]{1,0:T(8,128)S(1)} fusion(f32[256,1024]{1,0:T(8,128)} %bitcast.19, f32[32,2,8,512]{3,2,1,0:T(8,128)S(1)} %bitcast.75, s32[]{:T(128)S(6)} %select_n.31), kind=kOutput, calls=%fused_computation.12 | convolution fusion | flops 805306368 | bytes 3670020 | tf_op jit(solution)/shard_map/dot_general | solution.py:19
  149.0 3.7 %multiply_bitcast_fusion = f32[1,512,1024]{2,1,0:T(8,128)} fusion(f32[512,1024]{1,0:T(8,128)S(1)} %fusion.13, f32[256,1024]{1,0:T(8,128)} %collective-permute-done.3, f32[]{:T(128)} %bitcast.20, f32[32,2,8,512]{3,2,1,0:T(8,128)S(1)} %bitcast.76, s32[]{:T(128)S(6)} %select_n.35), kind=kOutput, calls=%fused_computation.8 | convolution fusion | flops 806354944 | bytes 5767176 | tf_op jit(solution)/shard_map/dot_general | solution.py:19
  (24 shorter events, 2.3 us)
Async XLA Ops:
  0.6 1.9 %copy-start = (f32[1,1,512,1024]{3,2,1,0:T(8,128)S(1)}, f32[1,1,512,1024]{3,2,1,0:T(8,128)}, u32[]{:S(2)}) copy-start(f32[1,1,512,1024]{3,2,1,0:T(8,128)} %param.5) | copy-start | bytes 6291460
  5.4 18.6 %collective-permute-start.1 = (f32[256,1024]{1,0:T(8,128)}, f32[256,1024]{1,0:T(8,128)}, u32[]{:S(2)}, u32[]{:S(2)}) collective-permute-start(f32[256,1024]{1,0:T(8,128)} %fusion.4), channel_id=1, source_target_pairs={{0,1},{1,0},{2,3},{3,2},{4,5},{5,4},{6,7},{7,6},{8,9},{9,8},{10,11... | collective-permute-start | bytes 3145736 | tf_op jit(solution)/shard_map/ppermute | solution.py:78
  23.3 7.4 %copy-start.2 = (f32[1,8,1024]{2,1,0:T(8,128)S(1)}, f32[1,8,1024]{2,1,0:T(8,128)}, u32[]{:S(2)}) copy-start(f32[1,8,1024]{2,1,0:T(8,128)} %param.7) | copy-start | bytes 98308
  23.3 7.4 %copy-start.3 = (f32[1,8,1024]{2,1,0:T(8,128)S(1)}, f32[1,8,1024]{2,1,0:T(8,128)}, u32[]{:S(2)}) copy-start(f32[1,8,1024]{2,1,0:T(8,128)} %param.6) | copy-start | bytes 98308
  26.4 22.9 %all-to-all-start = ((f32[16,16,1024]{2,1,0:T(8,128)}), f32[16,16,1024]{2,1,0:T(8,128)}, u32[]{:S(2)}, u32[]{:S(2)}) async-start(f32[16,16,1024]{2,1,0:T(8,128)} %bitcast.77), calls=%async_computation | async-start | bytes 2097152 | tf_op jit(solution)/shard_map/all_to_all | solution.py:79
  30.7 35.7 %collective-permute-start = (f32[16,1024]{1,0:T(8,128)S(1)}, f32[16,1024]{1,0:T(8,128)S(1)}, u32[]{:S(2)}, u32[]{:S(2)}) collective-permute-start(f32[16,1024]{1,0:T(8,128)S(1)} %pad_maximum_fusion), channel_id=1, source_target_pairs={{0,2},{2,0},{1,3},{3,1},{4,6},{6,4},{5,7},{7,5},{8,10},{10,8},{9,1... | collective-permute-start | bytes 196616 | tf_op jit(solution)/shard_map/ppermute | solution.py:83
  50.6 26.9 %copy-start.1 = (f32[1,2,512,512]{3,2,1,0:T(8,128)S(1)}, f32[1,2,512,512]{3,2,1,0:T(8,128)}, u32[]{:S(2)}) copy-start(f32[1,2,512,512]{3,2,1,0:T(8,128)} %param.9) | copy-start | bytes 6291460
  50.6 24.0 %collective-permute-start.2 = (f32[16,1024]{1,0:T(8,128)S(1)}, f32[16,1024]{1,0:T(8,128)S(1)}, u32[]{:S(2)}, u32[]{:S(2)}) collective-permute-start(f32[16,1024]{1,0:T(8,128)S(1)} %reduce_sum.36), channel_id=1, source_target_pairs={{0,2},{2,0},{1,3},{3,1},{4,6},{6,4},{5,7},{7,5},{8,10},{10,8},{9,1... | collective-permute-start | bytes 196616 | tf_op jit(solution)/shard_map/ppermute | solution.py:87
  96.3 52.7 %collective-permute-start.3 = (f32[256,1024]{1,0:T(8,128)}, f32[256,1024]{1,0:T(8,128)}, u32[]{:S(2)}, u32[]{:S(2)}) collective-permute-start(f32[256,1024]{1,0:T(8,128)} %bitcast.19), channel_id=1, source_target_pairs={{0,1},{1,0},{2,3},{3,2},{4,5},{5,4},{6,7},{7,6},{8,9},{9,8},{10,11... | collective-permute-start | bytes 3145736 | tf_op jit(solution)/shard_map/ppermute | solution.py:98
  110.4 11.3 %all-to-all-start.2 = ((f32[32,8,128]{2,1,0:T(8,128)}), f32[32,8,128]{2,1,0:T(8,128)S(1)}, u32[]{:S(2)}, u32[]{:S(2)}) async-start(f32[32,8,128]{2,1,0:T(8,128)} %broadcast_in_dim_broadcast_in_dim.3), calls=%async_computation.2 | async-start | bytes 262144 | tf_op jit(solution)/shard_map/all_to_all | solution.py:38
  121.8 13.1 %collective-permute-start.4 = (f32[8,128]{1,0:T(8,128)S(1)}, f32[8,128]{1,0:T(8,128)S(1)}, u32[]{:S(2)}, u32[]{:S(2)}) collective-permute-start(f32[8,128]{1,0:T(8,128)S(1)} %reduce_sum.38), channel_id=1, source_target_pairs={{0,514},{4,582},{8,650},{12,718},{16,786},{20,854},{24,922},{28,99... | collective-permute-start | bytes 12296 | tf_op jit(solution)/shard_map/ppermute | solution.py:54
  135.5 10.0 %all-to-all-start.3 = ((f32[16,8,128]{2,1,0:T(8,128)}), f32[16,8,128]{2,1,0:T(8,128)S(1)}, u32[]{:S(2)}, u32[]{:S(2)}) async-start(f32[16,8,128]{2,1,0:T(8,128)} %broadcast_in_dim.16), calls=%async_computation.3 | async-start | bytes 131072 | tf_op jit(solution)/shard_map/all_to_all | solution.py:38

commit v4 on v3

--- a/solution.py
+++ b/solution.py
@@ -26,11 +26,13 @@
     return out.reshape(values.shape)
 
 
-def right_back(values, basis):
-    blocks, order = basis.shape[0], basis.shape[1]
-    parts = values.reshape(values.shape[0], blocks, order)
-    out = jnp.einsum("rbd,bcd->rbc", parts, basis, precision=high)
-    return out.reshape(values.shape)
+def turned_blocks(values, left, basis):
+    blocks = basis.shape[0]
+    parts = jnp.split(values, blocks, axis=1)
+    return [
+        rows_dot(left, lax.dot_general(part, basis[b], (((1,), (1,)), ((), ())), precision=high))
+        for b, part in enumerate(parts)
+    ]
 
 
 def shared_total(tile, axes):
@@ -90,20 +92,20 @@
     new_second = 0.95 * second + 0.05 * mean * mean
     normal = new_first / (jnp.sqrt(new_second) + 1e-08)
 
-    squares = jnp.broadcast_to(jnp.sum(normal * normal), (8, 128))
-    expert_sum = shared_total(squares, PLANE_CORE)
-    turned = right_back(normal, right)
-    ours = lax.all_to_all(jnp.broadcast_to(turned, (chips, 2 * rows, width)), PLANE, 0, 0)
+    ours = lax.all_to_all(jnp.broadcast_to(normal, (chips, 2 * rows, width)), PLANE, 0, 0)
     ours = ours.reshape(-1, width)
     theirs = lax.ppermute(ours, "dp_3", SWAP)
-    another = along_z(expert_sum)
-    total = shared_total(another, PLANE)[0, 0]
+    squares = jnp.broadcast_to(jnp.sum(ours * ours), (8, 128))
+    another = along_z(squares)
+    total = shared_total(another, PLANE_CORE)[0, 0]
     count = lax.axis_size("expert") * order * width
     scale = jnp.sqrt(total / count + 1e-06)
-    back = rows_dot(here, ours)
-    back = back + rows_dot(there, theirs)
+    back = turned_blocks(ours, here, right)
+    more = turned_blocks(theirs, there, right)
+    back = lax.optimization_barrier([a + b for a, b in zip(back, more)])
+    back = jnp.concatenate([block * (1.0 / scale) for block in back], axis=1)
     own = lambda x: lax.dynamic_slice_in_dim(x, half * rows, rows, 0)
-    return ((back * (1.0 / scale))[None], own(new_first)[None], own(new_second)[None])
+    return (back[None], own(new_first)[None], own(new_second)[None])
 
 
 def solution(mesh):

time: 156 us -> 146 us (0.936); the launches traced: 153 us -> 145 us
  blocking collectives: 17.8 us -> 0 us
  matrix products: 14.5 us -> 20.7 us
  waiting for transfers between devices: 30.5 us -> 25.1 us
  starting transfers between devices: 79.5 us -> 83.8 us
  other arithmetic: 4.37 us -> 7.69 us
  local copies, waits for them, and re-layouts: 4.51 us -> 6.43 us
    all_to_all x1 -> x0, blocking collectives: 17.8 us -> none  [per_device(): lax.all_to_all(jnp.broadcast_to(turned, (chips, 2 * rows, width)), PLANE,...]
    all_to_all x0 -> x1, waiting for transfers between devices: none -> 11.2 us  [per_device(): lax.all_to_all(jnp.broadcast_to(normal, (chips, 2 * rows, width)), PLANE,...]
    all_to_all x2 -> x1, waiting for transfers between devices: 13.5 us -> 5.03 us  [shared_total(): return jnp.sum(lax.all_to_all(tiles, axes, 0, 0), axis=0)]
    ppermute x1, waiting for transfers between devices: 8.19 us -> 0.01 us  [along_z(): return lax.ppermute(tile, CHIPS, pairs)]
    dot_general x1 -> x4, matrix products: 0.92 us -> 8.14 us  [turned_blocks(): lax.dot_general(part, basis[b], (((1,), (1,)), ((), ())), precision=high)]
    all_to_all x0 -> x1, starting transfers between devices: none -> 6.16 us  [per_device(): lax.all_to_all(jnp.broadcast_to(normal, (chips, 2 * rows, width)), PLANE,...]
    ppermute x1, starting transfers between devices: 4.81 us -> 7.78 us  [along_z(): return lax.ppermute(tile, CHIPS, pairs)]
    ppermute x1, starting transfers between devices: 12.8 us -> 10.1 us  [per_device(): theirs = lax.ppermute(ours, 'dp_3', SWAP)]
  transfers between devices with their start and end apart: 8 -> 8, of which waited for: 5 -> 4; matrix products, arithmetic and copies ran while one was open for 6% -> 10% of each run, Pallas kernels for 0% -> 0%
where the time goes in v4:
time: 146 us; the launch traced here: 145 us
  starting transfers between devices  83.8 us (57%)
  waiting for transfers between devices  25.1 us (17%)
  matrix products  20.7 us (14%)
  other arithmetic  7.69 us (5%)
  local copies, waits for them, and re-layouts  6.43 us (4%)
  between operations  1.61 us (1%)
    ppermute x1, starting transfers between devices, per_device(): moments_there = lax.ppermute(moments, 'dp_2', SWAP)  18.5 us
    ppermute x1, starting transfers between devices, per_device(): pair = kept + lax.ppermute(sent, 'dp_3', SWAP)  16 us
    ppermute x1, starting transfers between devices, per_device(): summed = partial + lax.ppermute(partial, 'dp_2', SWAP)  15.6 us
    all_to_all x1, waiting for transfers between devices, per_device(): lax.all_to_all(jnp.broadcast_to(normal, (chips, 2 * rows, width)), PLANE,...  11.2 us
    ppermute x1, starting transfers between devices, per_device(): theirs = lax.ppermute(ours, 'dp_3', SWAP)  10.1 us
    ppermute x1, waiting for transfers between devices, per_device(): summed = partial + lax.ppermute(partial, 'dp_2', SWAP)  8.18 us
    dot_general x4, matrix products, turned_blocks(): lax.dot_general(part, basis[b], (((1,), (1,)), ((), ())), precision=high)  8.14 us
    ppermute x1, starting transfers between devices, along_z(): return lax.ppermute(tile, CHIPS, pairs)  7.78 us
  transfers between devices with their start and end apart: 8, of which 4 were waited for; matrix products, arithmetic and copies ran while one was open for 10% of the time, Pallas kernels for 0%

profile of v4, /device:TPU:1, one launch (start us, length us, event | category | flops | bytes accessed | tf_op | source)
XLA Modules:
  0.0 145.3 jit_solution(3070252121719766405)
XLA Ops:
  0.7 1.7 %copy.12 = f32[1,512,512]{1,2,0:T(8,128)S(1)} copy(f32[1,512,512]{2,1,0:T(8,128)} %param.8) | data formatting | bytes 2097152 | tf_op args[3]
  2.5 2.9 %fusion.2 = f32[256,1024]{1,0:T(8,128)} fusion(f32[1,1,512,1024]{3,2,1,0:T(8,128)S(1)} %copy-done, f32[32,2,8,512]{3,2,1,0:T(8,128)S(1)} %bitcast.72, s32[]{:T(128)S(6)} %select_n.35), kind=kOutput, calls=%fused_computation.3 | convolution fusion | flops 1610612736 | bytes 3670020 | tf_op jit(solution)/shard_map/dot_general | solution.py:78
  5.4 16.0 %collective-permute-start.1 = (f32[256,1024]{1,0:T(8,128)}, f32[256,1024]{1,0:T(8,128)}, u32[]{:S(2)}, u32[]{:S(2)}) collective-permute-start(f32[256,1024]{1,0:T(8,128)} %fusion.2), channel_id=1, source_target_pairs={{0,1},{1,0},{2,3},{3,2},{4,5},{5,4},{6,7},{7,6},{8,9},{9,8},{10,11... | collective-permute-start | bytes 3145736 | tf_op jit(solution)/shard_map/ppermute | solution.py:80
  21.4 1.9 %fusion.4 = f32[256,1024]{1,0:T(8,128)S(1)} fusion(f32[1,1,512,1024]{3,2,1,0:T(8,128)S(1)} %copy-done, f32[32,2,8,512]{3,2,1,0:T(8,128)S(1)} %bitcast.73, s32[]{:T(128)S(6)} %select_n.31), kind=kOutput, calls=%fused_computation.5 | convolution fusion | flops 1610612736 | bytes 3670020 | tf_op jit(solution)/shard_map/dot_general | solution.py:79
  24.0 2.3 %add.42 = f32[256,1024]{1,0:T(8,128)} add(f32[256,1024]{1,0:T(8,128)S(1)} %fusion.4, f32[256,1024]{1,0:T(8,128)} %collective-permute-done.1) | non-fusion elementwise | flops 262144 | bytes 3145728 | tf_op jit(solution)/shard_map/add | solution.py:80
  26.4 4.3 %all-to-all-start = ((f32[16,16,1024]{2,1,0:T(8,128)}), f32[16,16,1024]{2,1,0:T(8,128)}, u32[]{:S(2)}, u32[]{:S(2)}) async-start(f32[16,16,1024]{2,1,0:T(8,128)} %bitcast.78), calls=%async_computation | async-start | bytes 2097152 | tf_op jit(solution)/shard_map/all_to_all | solution.py:81
  30.7 18.5 %collective-permute-start = (f32[16,1024]{1,0:T(8,128)S(1)}, f32[16,1024]{1,0:T(8,128)S(1)}, u32[]{:S(2)}, u32[]{:S(2)}) collective-permute-start(f32[16,1024]{1,0:T(8,128)S(1)} %pad_maximum_fusion), channel_id=1, source_target_pairs={{0,2},{2,0},{1,3},{3,1},{4,6},{6,4},{5,7},{7,5},{8,10},{10,8},{9,1... | collective-permute-start | bytes 196616 | tf_op jit(solution)/shard_map/ppermute | solution.py:85
  50.6 15.6 %collective-permute-start.2 = (f32[16,1024]{1,0:T(8,128)S(1)}, f32[16,1024]{1,0:T(8,128)S(1)}, u32[]{:S(2)}, u32[]{:S(2)}) collective-permute-start(f32[16,1024]{1,0:T(8,128)S(1)} %reduce_sum.27), channel_id=1, source_target_pairs={{0,2},{2,0},{1,3},{3,1},{4,6},{6,4},{5,7},{7,5},{8,10},{10,8},{9,1... | collective-permute-start | bytes 196616 | tf_op jit(solution)/shard_map/ppermute | solution.py:89
  66.3 8.2 %collective-permute-done.2 = f32[16,1024]{1,0:T(8,128)S(1)} collective-permute-done((f32[16,1024]{1,0:T(8,128)S(1)}, f32[16,1024]{1,0:T(8,128)S(1)}, u32[]{:S(2)}, u32[]{:S(2)}) %collective-permute-start.2) | collective-permute-done | bytes 65568 | tf_op jit(solution)/shard_map/ppermute | solution.py:89
  74.5 2.2 %multiply_bitcast_fusion.1 = (f32[2,2,8,512]{3,2,1,0:T(8,128)S(1)}, f32[2,2,8,512]{3,2,1,0:T(8,128)S(1)}) fusion(f32[1,2,512,512]{3,2,1,0:T(8,128)} %param.9, f32[2,2,8,512]{3,2,1,0:T(8,128)S(1)} %bitcast.79), kind=kOutput, calls=%fused_computation.51 | convolution fusion | flops 50397184 | bytes 2293760 | tf_op jit(solution)/shard_map/rbc,bcd->rbd/dot_general | solution.py:25
  77.9 6.2 %all-to-all-start.1 = ((f32[16,16,1024]{2,1,0:T(8,128)}), f32[16,16,1024]{2,1,0:T(8,128)}, u32[]{:S(2)}, u32[]{:S(2)}) async-start(f32[16,16,1024]{2,1,0:T(8,128)} %broadcast_in_dim.18), calls=%async_computation.1 | async-start | bytes 2097152 | tf_op jit(solution)/shard_map/all_to_all | solution.py:95
  84.7 11.2 %all-to-all-done.1 = f32[16,16,1024]{2,1,0:T(8,128)} async-done(((f32[16,16,1024]{2,1,0:T(8,128)}), f32[16,16,1024]{2,1,0:T(8,128)}, u32[]{:S(2)}, u32[]{:S(2)}) %all-to-all-start.1) | async-done | bytes 1048608 | tf_op jit(solution)/shard_map/all_to_all | solution.py:95
  95.8 2.2 %multiply_reduce_fusion = f32[]{:T(128)} fusion(f32[16,16,1024]{2,1,0:T(8,128)} %all-to-all-done.1), kind=kLoop, calls=%fused_computation.17 | loop fusion | flops 524287 | bytes 1048580 | tf_op jit(solution)/shard_map/reduce_sum | solution.py:98
  98.7 7.8 %collective-permute-start.4 = (f32[8,128]{1,0:T(8,128)S(1)}, f32[8,128]{1,0:T(8,128)S(1)}, u32[]{:S(2)}, u32[]{:S(2)}) collective-permute-start(f32[8,128]{1,0:T(8,128)S(1)} %broadcast_in_dim.19), channel_id=1, source_target_pairs={{0,514},{4,582},{8,650},{12,718},{16,786},{20,854},{24,922},{28,99... | collective-permute-start | bytes 12296 | tf_op jit(solution)/shard_map/ppermute | solution.py:56
  106.5 10.1 %collective-permute-start.3 = (f32[256,1024]{1,0:T(8,128)}, f32[256,1024]{1,0:T(8,128)}, u32[]{:S(2)}, u32[]{:S(2)}) collective-permute-start(f32[256,1024]{1,0:T(8,128)} %bitcast.14), channel_id=1, source_target_pairs={{0,1},{1,0},{2,3},{3,2},{4,5},{5,4},{6,7},{7,6},{8,9},{9,8},{10,11... | collective-permute-start | bytes 3145736 | tf_op jit(solution)/shard_map/ppermute | solution.py:97
  116.7 2.0 %fusion.8 = f32[256,512]{1,0:T(8,128)S(1)} fusion(f32[1,2,512,512]{3,2,1,0:T(8,128)} %param.9, f32[256,1024]{1,0:T(8,128)} %bitcast.14), kind=kOutput, calls=%fused_computation.11 | convolution fusion | flops 402653184 | bytes 2097152 | tf_op jit(solution)/shard_map/dot_general | solution.py:33
  118.7 2.5 %fusion.12 = f32[256,512]{1,0:T(8,128)} fusion(f32[1,2,512,512]{3,2,1,0:T(8,128)S(1)} %copy-done.1, f32[256,1024]{1,0:T(8,128)} %bitcast.14), kind=kOutput, calls=%fused_computation.15 | convolution fusion | flops 402653184 | bytes 2097152 | tf_op jit(solution)/shard_map/dot_general | solution.py:33
  121.2 1.6 %fusion.25 = f32[512,512]{1,0:T(8,128)} fusion(f32[256,512]{1,0:T(8,128)S(1)} %fusion.8, f32[32,2,8,512]{3,2,1,0:T(8,128)S(1)} %bitcast.74, s32[]{:T(128)S(6)} %select_n.31), kind=kOutput, calls=%fused_computation.29 | convolution fusion | flops 402653184 | bytes 2097156 | tf_op jit(solution)/shard_map/dot_general | solution.py:19
  123.4 5.2 %all-to-all-start.2 = ((f32[32,8,128]{2,1,0:T(8,128)}), f32[32,8,128]{2,1,0:T(8,128)S(1)}, u32[]{:S(2)}, u32[]{:S(2)}) async-start(f32[32,8,128]{2,1,0:T(8,128)} %broadcast_in_dim.20), calls=%async_computation.2 | async-start | bytes 262144 | tf_op jit(solution)/shard_map/all_to_all | solution.py:40
  128.6 2.6 %fusion.27 = f32[512,512]{1,0:T(8,128)} fusion(f32[256,512]{1,0:T(8,128)} %fusion.12, f32[32,2,8,512]{3,2,1,0:T(8,128)S(1)} %bitcast.75, s32[]{:T(128)S(6)} %select_n.31), kind=kOutput, calls=%fused_computation.31 | convolution fusion | flops 402653184 | bytes 2097156 | tf_op jit(solution)/shard_map/dot_general | solution.py:19
  131.3 5.0 %all-to-all-done.2 = f32[32,8,128]{2,1,0:T(8,128)S(1)} async-done(((f32[32,8,128]{2,1,0:T(8,128)}), f32[32,8,128]{2,1,0:T(8,128)S(1)}, u32[]{:S(2)}, u32[]{:S(2)}) %all-to-all-start.2) | async-done | bytes 131104 | tf_op jit(solution)/shard_map/all_to_all | solution.py:40
  137.6 2.0 %fusion.10 = f32[256,512]{1,0:T(8,128)S(1)} fusion(f32[1,2,512,512]{3,2,1,0:T(8,128)} %param.9, f32[256,1024]{1,0:T(8,128)} %collective-permute-done.3), kind=kOutput, calls=%fused_computation.13 | convolution fusion | flops 402653184 | bytes 2097152 | tf_op jit(solution)/shard_map/dot_general | solution.py:33
  141.2 1.7 %fusion.6 = f32[256,512]{1,0:T(8,128)S(1)} fusion(f32[1,2,512,512]{3,2,1,0:T(8,128)S(1)} %copy-done.2, f32[256,1024]{1,0:T(8,128)} %collective-permute-done.3), kind=kOutput, calls=%fused_computation.9 | convolution fusion | flops 402653184 | bytes 2097152 | tf_op jit(solution)/shard_map/dot_general | solution.py:33
  143.8 1.5 %maximum_bitcast_fusion = f32[1,512,1024]{2,1,0:T(8,128)} fusion(f32[512,512]{1,0:T(8,128)S(1)} %get-tuple-element.20, f32[512,512]{1,0:T(8,128)S(1)} %get-tuple-element.21), kind=kLoop, calls=%fused_computation | loop fusion | flops 524288 | bytes 4194304 | tf_op jit(solution)/shard_map/broadcast_in_dim | solution.py:108
  (35 shorter events, 8.3 us)
Async XLA Ops:
  0.6 1.9 %copy-start = (f32[1,1,512,1024]{3,2,1,0:T(8,128)S(1)}, f32[1,1,512,1024]{3,2,1,0:T(8,128)}, u32[]{:S(2)}) copy-start(f32[1,1,512,1024]{3,2,1,0:T(8,128)} %param.5) | copy-start | bytes 6291460
  5.4 18.6 %collective-permute-start.1 = (f32[256,1024]{1,0:T(8,128)}, f32[256,1024]{1,0:T(8,128)}, u32[]{:S(2)}, u32[]{:S(2)}) collective-permute-start(f32[256,1024]{1,0:T(8,128)} %fusion.2), channel_id=1, source_target_pairs={{0,1},{1,0},{2,3},{3,2},{4,5},{5,4},{6,7},{7,6},{8,9},{9,8},{10,11... | collective-permute-start | bytes 3145736 | tf_op jit(solution)/shard_map/ppermute | solution.py:80
  23.3 7.4 %copy-start.5 = (f32[1,8,1024]{2,1,0:T(8,128)S(1)}, f32[1,8,1024]{2,1,0:T(8,128)}, u32[]{:S(2)}) copy-start(f32[1,8,1024]{2,1,0:T(8,128)} %param.7) | copy-start | bytes 98308
  23.3 7.4 %copy-start.6 = (f32[1,8,1024]{2,1,0:T(8,128)S(1)}, f32[1,8,1024]{2,1,0:T(8,128)}, u32[]{:S(2)}) copy-start(f32[1,8,1024]{2,1,0:T(8,128)} %param.6) | copy-start | bytes 98308
  26.4 22.9 %all-to-all-start = ((f32[16,16,1024]{2,1,0:T(8,128)}), f32[16,16,1024]{2,1,0:T(8,128)}, u32[]{:S(2)}, u32[]{:S(2)}) async-start(f32[16,16,1024]{2,1,0:T(8,128)} %bitcast.78), calls=%async_computation | async-start | bytes 2097152 | tf_op jit(solution)/shard_map/all_to_all | solution.py:81
  30.7 35.5 %collective-permute-start = (f32[16,1024]{1,0:T(8,128)S(1)}, f32[16,1024]{1,0:T(8,128)S(1)}, u32[]{:S(2)}, u32[]{:S(2)}) collective-permute-start(f32[16,1024]{1,0:T(8,128)S(1)} %pad_maximum_fusion), channel_id=1, source_target_pairs={{0,2},{2,0},{1,3},{3,1},{4,6},{6,4},{5,7},{7,5},{8,10},{10,8},{9,1... | collective-permute-start | bytes 196616 | tf_op jit(solution)/shard_map/ppermute | solution.py:85
  50.6 23.9 %collective-permute-start.2 = (f32[16,1024]{1,0:T(8,128)S(1)}, f32[16,1024]{1,0:T(8,128)S(1)}, u32[]{:S(2)}, u32[]{:S(2)}) collective-permute-start(f32[16,1024]{1,0:T(8,128)S(1)} %reduce_sum.27), channel_id=1, source_target_pairs={{0,2},{2,0},{1,3},{3,1},{4,6},{6,4},{5,7},{7,5},{8,10},{10,8},{9,1... | collective-permute-start | bytes 196616 | tf_op jit(solution)/shard_map/ppermute | solution.py:89
  77.9 18.0 %all-to-all-start.1 = ((f32[16,16,1024]{2,1,0:T(8,128)}), f32[16,16,1024]{2,1,0:T(8,128)}, u32[]{:S(2)}, u32[]{:S(2)}) async-start(f32[16,16,1024]{2,1,0:T(8,128)} %broadcast_in_dim.18), calls=%async_computation.1 | async-start | bytes 2097152 | tf_op jit(solution)/shard_map/all_to_all | solution.py:95
  95.8 22.9 %copy-start.1 = (f32[1,2,512,512]{3,2,1,0:T(8,128)S(1)}, f32[1,2,512,512]{3,2,1,0:T(8,128)}, u32[]{:S(2)}) copy-start(f32[1,2,512,512]{3,2,1,0:T(8,128)} %param.9) | copy-start | bytes 6291460
  98.7 24.0 %collective-permute-start.4 = (f32[8,128]{1,0:T(8,128)S(1)}, f32[8,128]{1,0:T(8,128)S(1)}, u32[]{:S(2)}, u32[]{:S(2)}) collective-permute-start(f32[8,128]{1,0:T(8,128)S(1)} %broadcast_in_dim.19), channel_id=1, source_target_pairs={{0,514},{4,582},{8,650},{12,718},{16,786},{20,854},{24,922},{28,99... | collective-permute-start | bytes 12296 | tf_op jit(solution)/shard_map/ppermute | solution.py:56
  106.5 31.1 %collective-permute-start.3 = (f32[256,1024]{1,0:T(8,128)}, f32[256,1024]{1,0:T(8,128)}, u32[]{:S(2)}, u32[]{:S(2)}) collective-permute-start(f32[256,1024]{1,0:T(8,128)} %bitcast.14), channel_id=1, source_target_pairs={{0,1},{1,0},{2,3},{3,2},{4,5},{5,4},{6,7},{7,6},{8,9},{9,8},{10,11... | collective-permute-start | bytes 3145736 | tf_op jit(solution)/shard_map/ppermute | solution.py:97
  123.4 12.9 %all-to-all-start.2 = ((f32[32,8,128]{2,1,0:T(8,128)}), f32[32,8,128]{2,1,0:T(8,128)S(1)}, u32[]{:S(2)}, u32[]{:S(2)}) async-start(f32[32,8,128]{2,1,0:T(8,128)} %broadcast_in_dim.20), calls=%async_computation.2 | async-start | bytes 262144 | tf_op jit(solution)/shard_map/all_to_all | solution.py:40
  136.4 3.3 %copy-start.4 = (f32[512,512]{1,0:T(8,128)S(1)}, f32[512,512]{1,0:T(8,128)}, u32[]{:S(2)}) copy-start(f32[512,512]{1,0:T(8,128)} %fusion.27) | copy-start | bytes 3145732
  139.6 1.6 %copy-start.2 = (f32[1,2,512,512]{3,2,1,0:T(8,128)S(1)}, f32[1,2,512,512]{3,2,1,0:T(8,128)}, u32[]{:S(2)}) copy-start(f32[1,2,512,512]{3,2,1,0:T(8,128)} %param.9) | copy-start | bytes 6291460
  139.6 3.3 %copy-start.3 = (f32[512,512]{1,0:T(8,128)S(1)}, f32[512,512]{1,0:T(8,128)}, u32[]{:S(2)}) copy-start(f32[512,512]{1,0:T(8,128)} %fusion.25) | copy-start | bytes 3145732
